TPU v7x, 32 devices: a whole 2x2x4 slice. The times are simulated.
32 devices in a mesh: leaf: 8 (over z, y), probe: 4 (over x, core).
Axes of the slice: x: 2, y: 2, z: 4, core: 2. Of those that a mesh axis runs over, the one named last changes fastest.
Arguments:
- coords: float32 [3, 32768], P(None, 'leaf')
- site_order: int32 [128, 256], P('leaf'), may hold values from 0 to 255, each once within a row
- leaf_pairs: int32 [2, 768], P(None, 'leaf'), may hold values from 0 to 127, as said below
- pair_count: int32 [8], P('leaf'), may hold values from 31 to 96, as said below
- probes: float32 [64, 32768], P('probe', 'leaf'), may hold values from -16 to 16
Outputs:
- solution: float32 [64, 32768], P('probe', 'leaf')
- residual: float32 [64, 32768], P('probe', 'leaf')
Inputs may be any that keep to these rules, and one draw needn't show every extreme that they name: `leaf_pairs`: each leaf index owns 96 slots; its first pair_count slots hold distinct pairs (i, j) with i among that index's own 16 leaves and i <= j <= i + 5, j < 128, every own leaf listed with itself once and with the next leaf where there is one; the later slots hold the index's first leaf twice. `pair_count`: pairs listed for each leaf index; some index lists 96 in every draw. Each row of site_order lists 0 to 255 once.
All inputs are finite; a program needn't handle non-finite values.
Results may differ from a plain program's by a relative error of at most 0.0003.
Values sent between devices are 32-bit elements; how exact they have to be, the bound alone decides.
A program may use at most 64 MiB of HBM per device.

v0:
```python
import functools
import math

import jax
import jax.numpy as jnp
from jax import lax
from jax.experimental import pallas as pl
from jax.experimental.pallas import tpu as pltpu
from jax.sharding import PartitionSpec as P

REACH = 5
UNIT = 0.025
LENGTH = 0.12
NUGGET = 0.5
TAPER = REACH * UNIT
GROW = math.sqrt(3.0) * TAPER / LENGTH
QUAD = 4.0 * GROW
LIN = (4.0 + GROW) / QUAD
RATE = -GROW / math.log(2.0)
OFFS = REACH + 1
ROWS = 32
MESH = pl.DeviceIdType.MESH
F32 = jnp.float32
BF16 = jnp.bfloat16


def split(x):
    hi = x.astype(BF16)
    return hi, (x - hi.astype(F32)).astype(BF16)


def stacked(x):
    hi = x.astype(BF16).astype(F32)
    return jnp.concatenate([hi, x - hi], axis=0).astype(BF16)


def dot(a, b, ca, cb):
    return lax.dot_general(a, b, (((ca,), (cb,)), ((), ())), preferred_element_type=F32)


def fold(x):
    half = x.shape[0] // 2
    return x[:half] + x[half:]


def kernel(
    n, coords_ref, order_ref, pairs_ref, count_ref, probes_ref, sol_ref, res_ref,
    c8, prow, pcb, mask, tiles, v, v2, acc, r1, acc2, twin0, twin1, halo0, halo1,
    part0, part1, back0, back1, sum_out, sum_in, ssem, rsem, hsend, hrecv,
):
    leaf_dev, width = order_ref.shape
    cols = probes_ref.shape[0]
    half = leaf_dev // 2
    span = half + REACH
    me = lax.axis_index("leaf")
    probe = lax.axis_index("probe")
    mine = lax.rem(probe, 2)
    other = 1 - mine
    even = probe - mine
    twin = even + other
    base = half * mine
    twin_base = half * other
    after = lax.rem(me + 1, n)
    before = lax.rem(me + n - 1, n)

    peers = [(k - 1, lax.rem(me + k, n), probe, mine) for k in range(1, n)]
    peers += [(n - 1 + k, lax.rem(me + k, n), twin, other) for k in range(n)]
    slots_in = len(peers)

    barrier = pltpu.get_barrier_semaphore()
    for _, leaf, row, _ in peers:
        pl.semaphore_signal(
            barrier, inc=1, device_id={"leaf": leaf, "probe": row}, device_id_type=MESH
        )

    rr = jnp.zeros((cols, width), F32)
    for l in range(leaf_dev):
        x = probes_ref[:, l * width : (l + 1) * width]
        v[mine, l] = x
        rr = rr + x * x
    v[mine, pl.ds(leaf_dev, REACH)] = jnp.zeros((REACH, cols, width), F32)

    c8[...] = jnp.zeros_like(c8)
    c8[0:3, :] = coords_ref[...] * (1.0 / TAPER)
    place = lax.broadcasted_iota(jnp.int32, (width, width), 0)

    for l in range(leaf_dev):
        x = c8[:, l * width : (l + 1) * width]
        hi = x.astype(BF16).astype(F32)
        mid = (x - hi).astype(BF16).astype(F32)
        parts = jnp.concatenate([hi, mid, x - hi - mid], axis=0).astype(BF16)
        onehot = jnp.where(place == order_ref[l : l + 1, :], 1.0, 0.0).astype(BF16)
        got = dot(parts, onehot, 1, 0)
        prow[l] = got[0:8] + got[8:16] + got[16:24]

    pl.semaphore_wait(barrier, slots_in)

    def hop(src, dst, slot, leaf, row, landing=None):
        return pltpu.make_async_remote_copy(
            src_ref=src, dst_ref=dst, send_sem=hsend.at[slot],
            recv_sem=hrecv.at[slot if landing is None else landing],
            device_id={"leaf": leaf, "probe": row}, device_id_type=MESH,
        )

    twin0_hop = hop(v.at[mine, pl.ds(twin_base, span)], twin0, 0, me, twin)
    point_hop = hop(prow.at[pl.ds(0, REACH)], prow.at[pl.ds(leaf_dev, REACH)], 1, before, probe)
    rim0_hop = hop(v.at[mine, pl.ds(0, REACH)], halo0.at[mine], 2, before, even + 1, 2 + mine)
    rim0_in = [
        hop(v.at[mine, pl.ds(0, REACH)], halo0.at[k], 2, before, even + 1, 2 + k) for k in range(2)
    ]
    twin0_hop.start()
    point_hop.start()

    @pl.when(me > 0)
    def _():
        rim0_hop.start()


    slots = pairs_ref.shape[1]
    first = pairs_ref[0:1, :]
    second = pairs_ref[1:2, :]
    code = (first - me * leaf_dev) * OFFS + (second - first)
    lane = lax.broadcasted_iota(jnp.int32, (1, slots), 1)
    code = jnp.where(lane < count_ref[0], code, -1)
    want = lax.broadcasted_iota(jnp.int32, (leaf_dev * OFFS, slots), 0)
    hit = jnp.max(jnp.where(want == code, 1.0, 0.0), axis=1, keepdims=True)
    mask[...] = jnp.broadcast_to(hit, mask.shape)
    acc[...] = jnp.zeros_like(acc)
    acc2[...] = jnp.zeros_like(acc2)

    def both(field, l):
        return stacked(jnp.concatenate([field[0, l], field[1, l]], axis=0))

    def accept(field, twins):
        for k in range(span):
            field[other, base + k] = twins[k]
        for k in range(span):
            v2[base + k] = both(field, base + k)

    def accept_rim(field, halo):
        for k in range(REACH):
            for r in range(2):
                field[r, leaf_dev + k] = halo[r, k]
            v2[leaf_dev + k] = both(field, leaf_dev + k)

    def add(into, l, x):
        x = fold(x)
        into[0, l] += x[:cols]
        into[1, l] += x[cols:]

    def products(i, get, into):
        vi = v2[i]
        row = jnp.zeros((width, 4 * cols), F32)
        for o in range(OFFS):
            hi, lo = get((i - base) * OFFS + o, o)
            vj = v2[i + o]
            row = row + dot(hi, vj, 1, 1) + dot(lo, vj, 1, 1)
            if o > 0:
                add(into, i + o, dot(vi, hi, 1, 0) + dot(vi, lo, 1, 0))
        add(into, i, row.T)

    def build(i, s, o):
        for h in range(0, width, 128):
            listed = mask[pl.ds(i * OFFS + o, 1), :]
            right = [
                jnp.broadcast_to(
                    jnp.where(
                        listed > 0.0,
                        prow[i + o, c : c + 1, h : h + 128],
                        prow[i, c : c + 1, h : h + 128],
                    ),
                    (ROWS, 128),
                )
                for c in range(3)
            ]
            top = jnp.broadcast_to(listed, (ROWS, 128))
            for a in range(0, width, ROWS):
                dx = pcb[0, a : a + ROWS, :] - right[0]
                dy = pcb[1, a : a + ROWS, :] - right[1]
                dz = pcb[2, a : a + ROWS, :] - right[2]
                d2 = jnp.maximum(dx * dx + dy * dy + dz * dz, 1e-30)
                u = d2 * lax.rsqrt(d2)
                w = jnp.maximum(top - u, 0.0)
                w = w * w
                w = w * w
                t = w * (d2 + (LIN * u + 1.0 / QUAD)) * jnp.exp2(RATE * u)
                hi, lo = split(t)
                tiles[s, 0, a : a + ROWS, h : h + 128] = hi
                tiles[s, 1, a : a + ROWS, h : h + 128] = lo
        return tiles[s, 0], tiles[s, 1]

    @pl.when(me == n - 1)
    def _():
        halo0[...] = jnp.zeros_like(halo0)
        halo1[...] = jnp.zeros_like(halo1)

    twin0_hop.wait_recv()
    accept(v, twin0)

    def first_pass(i, carry):
        @pl.when(i == leaf_dev - REACH)
        def _():
            point_hop.wait_recv()
            @pl.when(me < n - 1)
            def _():
                for k in range(2):
                    rim0_in[k].wait_recv()

            accept_rim(v, halo0)

        turned = prow[i].T
        for c in range(3):
            pcb[c] = jnp.broadcast_to(turned[:, c : c + 1], (width, 128))
        products(i, lambda s, o: build(i, s, o), acc)
        return carry

    lax.fori_loop(base, base + half, first_pass, 0)

    @pl.when(mine == 0)
    def _():
        point_hop.wait_recv()

    lanes = lax.broadcasted_iota(jnp.int32, (cols, 128), 1)

    def overlap(field, sums):
        totals = []
        for r in range(2):
            x = jnp.zeros((cols, width), F32)
            for k in range(span):
                x = x + field[r, base + k] * sums[r, base + k]
            totals.append(jnp.sum(x, axis=1, keepdims=True))
        return totals

    def share(which, shared, own):
        own = [jnp.sum(x, axis=1, keepdims=True) for x in own]
        for r in range(2):
            keep = jnp.where(mine == r, 1.0, 0.0)
            packed = jnp.where(lanes == 0, shared[r], 0.0)
            for k, x in enumerate(own):
                packed = jnp.where(lanes == k + 1, x * keep, packed)
            sum_out[which, r] = packed
        copies = []
        for slot, leaf, row, side in peers:
            at = which * slots_in + slot
            copy = pltpu.make_async_remote_copy(
                src_ref=sum_out.at[which, side], dst_ref=sum_in.at[at],
                send_sem=ssem.at[at], recv_sem=rsem.at[at],
                device_id={"leaf": leaf, "probe": row}, device_id_type=MESH,
            )
            copy.start()
            copies.append(copy)
        return copies

    def collect(which, copies):
        total = sum_out[which, mine]
        for k, copy in enumerate(copies):
            copy.wait()
            total = total + sum_in[which * slots_in + k]
        return total

    def give_back(sums, part, back, slot):
        whole = hop(sums.at[other, pl.ds(base, span)], part, slot, me, twin)
        rims = [
            hop(sums.at[r, pl.ds(leaf_dev, REACH)], back, slot + 1 + r, after, even + r, slot + 1)
            for r in range(2)
        ]
        whole.start()

        @pl.when(jnp.logical_and(mine == 1, me < n - 1))
        def _():
            for rim in rims:
                rim.start()

        return whole, rims

    def take_back(sums, part, back, hops):
        whole, rims = hops
        whole.wait_recv()
        for k in range(span):
            sums[mine, twin_base + k] += part[k]

        @pl.when(me > 0)
        def _():
            rims[0].wait_recv()
            for k in range(REACH):
                sums[mine, k] += back[k]

        whole.wait_send()

        @pl.when(jnp.logical_and(mine == 1, me < n - 1))
        def _():
            for rim in rims:
                rim.wait_send()

    copies = share(0, overlap(v, acc), [rr])
    hops = give_back(acc, part0, back0, 4)
    total = collect(0, copies)
    rr0 = total[:, 1:2]
    dq0 = total[:, 0:1] * QUAD + NUGGET * rr0
    alpha0 = rr0 / dq0
    take_back(acc, part0, back0, hops)

    rr1 = jnp.zeros((cols, width), F32)
    rq = jnp.zeros((cols, width), F32)
    for l in range(leaf_dev):
        d = v[mine, l]
        q = NUGGET * d + QUAD * acc[mine, l]
        r = d - alpha0 * q
        acc[mine, l] = q
        r1[mine, l] = r
        rr1 = rr1 + r * r
        rq = rq + r * q
    r1[mine, pl.ds(leaf_dev, REACH)] = jnp.zeros((REACH, cols, width), F32)
    twin1_hop = hop(r1.at[mine, pl.ds(twin_base, span)], twin1, 7, me, twin)
    rim1_hop = hop(r1.at[mine, pl.ds(0, REACH)], halo1.at[mine], 8, before, even + 1, 8 + mine)
    rim1_in = [
        hop(r1.at[mine, pl.ds(0, REACH)], halo1.at[k], 8, before, even + 1, 8 + k) for k in range(2)
    ]
    twin1_hop.start()

    @pl.when(me > 0)
    def _():
        rim1_hop.start()

    twin1_hop.wait()
    accept(r1, twin1)

    def second_pass(i, carry):
        @pl.when(i == leaf_dev - REACH)
        def _():
            @pl.when(me < n - 1)
            def _():
                for k in range(2):
                    rim1_in[k].wait_recv()

            accept_rim(r1, halo1)

        products(i, lambda s, o: (tiles[s, 0], tiles[s, 1]), acc2)
        return carry

    lax.fori_loop(base, base + half, second_pass, 0)

    copies = share(1, overlap(r1, acc2), [rr1, rq])
    hops = give_back(acc2, part1, back1, 10)
    total = collect(1, copies)
    new = total[:, 1:2]
    beta = new / rr0
    curve = total[:, 0:1] * QUAD + NUGGET * new + beta * (2.0 * total[:, 2:3] + beta * dq0)
    alpha1 = new / curve
    take_back(acc2, part1, back1, hops)
    for l in range(leaf_dev):
        d = v[mine, l]
        r = r1[mine, l]
        q = NUGGET * r + QUAD * acc2[mine, l] + beta * acc[mine, l]
        sol_ref[:, l * width : (l + 1) * width] = alpha0 * d + alpha1 * (r + beta * d)
        res_ref[:, l * width : (l + 1) * width] = r - alpha1 * q
    for copy in (twin0_hop, point_hop):
        copy.wait_send()

    @pl.when(me > 0)
    def _():
        rim0_hop.wait_send()
        rim1_hop.wait_send()


def body(coords, site_order, leaf_pairs, pair_count, probes):
    n = lax.axis_size("leaf")
    leaf_dev, width = site_order.shape
    cols = probes.shape[0]
    extent = leaf_dev + REACH
    span = leaf_dev // 2 + REACH
    slots_in = 2 * n - 1
    vmem = pl.BlockSpec(memory_space=pltpu.VMEM)
    smem = pl.BlockSpec(memory_space=pltpu.SMEM)
    field = functools.partial(pltpu.VMEM, dtype=F32)
    return pl.pallas_call(
        functools.partial(kernel, n),
        out_shape=(jax.ShapeDtypeStruct(probes.shape, F32),) * 2,
        in_specs=[vmem, vmem, vmem, smem, vmem],
        out_specs=(vmem, vmem),
        scratch_shapes=[
            field((8, leaf_dev * width)),
            field((extent, 8, width)),
            field((3, width, 128)),
            field((leaf_dev * OFFS, 128)),
            pltpu.VMEM((leaf_dev // 2 * OFFS, 2, width, width), BF16),
            field((2, extent, cols, width)),
            pltpu.VMEM((extent, 4 * cols, width), BF16),
            field((2, extent, cols, width)),
            field((2, extent, cols, width)),
            field((2, extent, cols, width)),
            field((span, cols, width)),
            field((span, cols, width)),
            field((2, REACH, cols, width)),
            field((2, REACH, cols, width)),
            field((span, cols, width)),
            field((span, cols, width)),
            field((REACH, cols, width)),
            field((REACH, cols, width)),
            field((2, 2, cols, 128)),
            field((2 * slots_in, cols, 128)),
            pltpu.SemaphoreType.DMA((2 * slots_in,)),
            pltpu.SemaphoreType.DMA((2 * slots_in,)),
            pltpu.SemaphoreType.DMA((13,)),
            pltpu.SemaphoreType.DMA((13,)),
        ],
        compiler_params=pltpu.CompilerParams(
            collective_id=0, has_side_effects=True, vmem_limit_bytes=48 * 2**20
        ),
    )(coords, site_order, leaf_pairs, pair_count, probes)


def solution(mesh):
    in_specs = (P(None, "leaf"), P("leaf", None), P(None, "leaf"), P("leaf"), P("probe", "leaf"))
    out_specs = (P("probe", "leaf"), P("probe", "leaf"))
    return jax.shard_map(body, mesh=mesh, in_specs=in_specs, out_specs=out_specs, check_vma=False)
```

profile of v0, /device:TPU:0, one launch (start us, length us, event | category | flops | bytes accessed | tf_op | source)
XLA Modules:
  0.0 48.4 jit_solution(3427184883438660582)
XLA Ops:
  0.6 0.0 copy-start.3
  1.3 0.0 copy-done.3
  1.3 0.0 copy-start
  1.3 0.9 %copy-done = f32[16,4096]{1,0:T(8,128)S(1)} copy-done((f32[16,4096]{1,0:T(8,128)S(1)}, f32[16,4096]{1,0:T(8,128)}, u32[]{:S(2)}) %copy-start) | copy-done | bytes 262168
  2.3 0.0 copy-start.1
  2.3 0.8 %copy-done.1 = f32[3,4096]{1,0:T(4,128)S(1)} copy-done((f32[3,4096]{1,0:T(4,128)S(1)}, f32[3,4096]{1,0:T(4,128)}, u32[]{:S(2)}) %copy-start.1) | copy-done | bytes 49176
  3.1 0.0 copy-start.2
  3.1 0.7 %copy-done.2 = s32[16,256]{1,0:T(8,128)S(1)} copy-done((s32[16,256]{1,0:T(8,128)S(1)}, s32[16,256]{1,0:T(8,128)}, u32[]{:S(2)}) %copy-start.2) | copy-done | bytes 16408
  3.8 43.2 %shard_map.68 = (f32[16,4096]{1,0:T(8,128)S(1)}, f32[16,4096]{1,0:T(8,128)S(1)}) custom-call(f32[3,4096]{1,0:T(4,128)S(1)} %copy-done.1, s32[16,256]{1,0:T(8,128)S(1)} %copy-done.2, s32[2,96]{1,0:T(2,128)S(1)} %copy-done.3, s32[1]{0:T(128)S(6)} %copy.9.count_ref, f32[16,4096]{1,0:T(8,128)S(1)} %copy-done), custom_call_target="tpu_custom_call" | custom-call | tf_op jit(solution)/shard_map/pallas_call | solution.py:376
  47.0 0.7 %copy.10 = f32[16,4096]{1,0:T(8,128)} copy(f32[16,4096]{1,0:T(8,128)S(1)} %get-tuple-element.4) | data formatting | bytes 524288
  47.7 0.7 %copy.11 = f32[16,4096]{1,0:T(8,128)} copy(f32[16,4096]{1,0:T(8,128)S(1)} %get-tuple-element.5) | data formatting | bytes 524288
Async XLA Ops:
  0.6 0.7 %copy-start.3 = (s32[2,96]{1,0:T(2,128)S(1)}, s32[2,96]{1,0:T(2,128)}, u32[]{:S(2)}) copy-start(s32[2,96]{1,0:T(2,128)} %pairs_ref.1) | copy-start | bytes 2308
  1.3 0.9 %copy-start = (f32[16,4096]{1,0:T(8,128)S(1)}, f32[16,4096]{1,0:T(8,128)}, u32[]{:S(2)}) copy-start(f32[16,4096]{1,0:T(8,128)} %probes_ref.1) | copy-start | bytes 786436
  2.3 0.8 %copy-start.1 = (f32[3,4096]{1,0:T(4,128)S(1)}, f32[3,4096]{1,0:T(4,128)}, u32[]{:S(2)}) copy-start(f32[3,4096]{1,0:T(4,128)} %coords_ref.1) | copy-start | bytes 147460
  3.1 0.7 %copy-start.2 = (s32[16,256]{1,0:T(8,128)S(1)}, s32[16,256]{1,0:T(8,128)}, u32[]{:S(2)}) copy-start(s32[16,256]{1,0:T(8,128)} %order_ref.1) | copy-start | bytes 49156
where the time goes:
time: 48.7 us; the launch traced here: 48.4 us
  Pallas kernels  43.2 us (89%)
  local copies, waits for them, and re-layouts  3.92 us (8%)
  between operations  1.32 us (3%)
    pallas_call x1, Pallas kernels, body(): pl.pallas_call(functools.partial(kernel, n), out_shape=(jax.ShapeDtypeStr...  43.2 us
    unnamed x10, local copies, waits for them, and re-layouts  3.92 us

commit v1 on v0

v1 whole, which is shorter than its diff:
```python
import functools
import math

import jax
import jax.numpy as jnp
from jax import lax
from jax.experimental import pallas as pl
from jax.experimental.pallas import tpu as pltpu
from jax.sharding import PartitionSpec as P

REACH = 5
UNIT = 0.025
LENGTH = 0.12
NUGGET = 0.5
SHIFT = NUGGET + 1.0
TAPER = REACH * UNIT
GROW = math.sqrt(3.0) * TAPER / LENGTH
RATE = GROW / math.log(2.0)
QUAD = 4.0 * GROW
LIN = -(4.0 + 9.0 * GROW) * RATE / QUAD
CON = 5.0 * (1.0 + GROW) * RATE**2 / QUAD
NORM = QUAD * 2.0**-RATE / RATE**6
OFFS = REACH + 1
ROWS = 32
MESH = pl.DeviceIdType.MESH
F32 = jnp.float32
BF16 = jnp.bfloat16


def dot(a, b, ca, cb):
    return lax.dot_general(a, b, (((ca,), (cb,)), ((), ())), preferred_element_type=F32)


def three(x, axis):
    hi = x.astype(BF16).astype(F32)
    mid = (x - hi).astype(BF16).astype(F32)
    return jnp.concatenate([hi, mid, x - hi - mid], axis=axis).astype(BF16)


def kernel(
    n, coords_hbm, order_hbm, pairs_hbm, count_hbm, probes_hbm, sol_ref, res_ref,
    cin, order, pairs, count, own, c8, prow, pcb, mask, tiles, d, w, wfar, v2, acc, acc2,
    in_low, in_high, part, back, sum_out, sum_in, isem, ssem, rsem, hsend, hrecv,
):
    leaf_dev, width = order.shape
    cols = probes_hbm.shape[0]
    half = leaf_dev // 2
    span = half + REACH
    me = lax.axis_index("leaf")
    probe = lax.axis_index("probe")
    mine = lax.rem(probe, 2)
    other = 1 - mine
    even = probe - mine
    twin = even + other
    base = half * mine
    twin_base = half * other
    after = lax.rem(me + 1, n)
    before = lax.rem(me + n - 1, n)
    low_leaf = jnp.where(mine == 0, before, me)
    high_leaf = jnp.where(mine == 0, me, after)
    has_low = jnp.logical_or(mine == 1, me > 0)
    has_high = jnp.logical_or(mine == 0, me < n - 1)

    peers = [(k - 1, lax.rem(me + k, n), probe) for k in range(1, n)]
    peers += [(n - 1 + k, lax.rem(me + k, n), twin) for k in range(n)]
    slots_in = len(peers)

    def load(src, dst, slot):
        return pltpu.make_async_copy(src, dst, isem.at[slot])

    loads = [
        load(coords_hbm, cin, 0), load(order_hbm, order, 1), load(pairs_hbm, pairs, 2),
        load(count_hbm, count, 3),
    ]
    for l in range(leaf_dev):
        loads.append(load(probes_hbm.at[:, l * width : (l + 1) * width], own.at[l], 4 + l))
    for copy in loads:
        copy.start()
    barrier = pltpu.get_barrier_semaphore()
    for _, leaf, row in peers:
        pl.semaphore_signal(
            barrier, inc=1, device_id={"leaf": leaf, "probe": row}, device_id_type=MESH
        )

    def hop(src, dst, slot, leaf, row, landing=None):
        return pltpu.make_async_remote_copy(
            src_ref=src, dst_ref=dst, send_sem=hsend.at[slot],
            recv_sem=hrecv.at[slot if landing is None else landing],
            device_id={"leaf": leaf, "probe": row}, device_id_type=MESH,
        )

    place = lax.broadcasted_iota(jnp.int32, (width, width), 0)
    for copy in loads[:4]:
        copy.wait()
    c8[...] = jnp.zeros_like(c8)
    c8[0:3, :] = cin[...] * (RATE / TAPER)

    def gather(k):
        x = c8[:, pl.ds(pl.multiple_of((base + k) * width, width), width)]
        parts = three(x, 0)
        onehot = jnp.where(place == order[pl.ds(base + k, 1), :], 1.0, 0.0).astype(BF16)
        got = dot(parts, onehot, 1, 0)
        prow[k] = got[0:8] + got[8:16] + got[16:24]

    for k in range(half):
        gather(k)

    @pl.when(mine == 0)
    def _():
        for k in range(half, span):
            gather(k)

    slots = pairs.shape[1]
    first = pairs[0:1, :]
    second = pairs[1:2, :]
    code = (first - me * leaf_dev - base) * OFFS + (second - first)
    lane = lax.broadcasted_iota(jnp.int32, (1, slots), 1)
    code = jnp.where(lane < count[0], code, -1)
    want = lax.broadcasted_iota(jnp.int32, (half * OFFS, slots), 0)
    hit = jnp.max(jnp.where(want == code, RATE, 0.0), axis=1, keepdims=True)
    mask[...] = jnp.broadcast_to(hit, mask.shape)
    acc[...] = jnp.zeros_like(acc)
    acc2[...] = jnp.zeros_like(acc2)

    def both(field, k):
        return jnp.concatenate([field[0, k], field[1, k]], axis=0)

    def stack(k, x):
        hi = x.astype(BF16)
        v2[k] = jnp.concatenate([hi, (x - hi.astype(F32)).astype(BF16)], axis=0)

    def add(into, k, x):
        into[0, k] += x[:cols]
        into[1, k] += x[cols:]

    rows = 2 * cols

    def products(i, into):
        vi = v2[i]
        row = jnp.zeros((2 * rows, width), F32)
        low = jnp.zeros((rows, width), F32)
        for o in range(OFFS):
            hi = tiles[i * OFFS + o, 0]
            lo = tiles[i * OFFS + o, 1]
            vj = v2[i + o]
            row = row + dot(vj, hi, 1, 1)
            low = low + dot(vj[:rows], lo, 1, 1)
            if o > 0:
                col = dot(vi, hi, 1, 0)
                add(into, i + o, col[:rows] + col[rows:] + dot(vi[:rows], lo, 1, 0))
        add(into, i, row[:rows] + row[rows:] + low)

    def build(i):
        turned = prow[i].T
        for c in range(3):
            pcb[c] = jnp.broadcast_to(turned[:, c : c + 1], (width, 128))
        for o in range(OFFS):
            s = i * OFFS + o
            for h in range(0, width, 128):
                listed = mask[pl.ds(s, 1), :]
                right = [
                    jnp.broadcast_to(
                        jnp.where(
                            listed > 0.0,
                            prow[i + o, c : c + 1, h : h + 128],
                            prow[i, c : c + 1, h : h + 128],
                        ),
                        (ROWS, 128),
                    )
                    for c in range(3)
                ]
                top = jnp.broadcast_to(listed, (ROWS, 128))
                for a in range(0, width, ROWS):
                    dx = pcb[0, a : a + ROWS, :] - right[0]
                    dy = pcb[1, a : a + ROWS, :] - right[1]
                    dz = pcb[2, a : a + ROWS, :] - right[2]
                    d2 = jnp.maximum(dx * dx + dy * dy + dz * dz, 1e-30)
                    y = jnp.maximum(top - d2 * lax.rsqrt(d2), 0.0)
                    y2 = y * y
                    t = (y2 * y2) * (y2 + (LIN * y + CON)) * jnp.exp2(y)
                    hi = t.astype(BF16)
                    tiles[s, 0, a : a + ROWS, h : h + 128] = hi
                    tiles[s, 1, a : a + ROWS, h : h + 128] = (t - hi.astype(F32)).astype(BF16)

    build(0)

    for copy in loads[4:]:
        copy.wait()
    pl.semaphore_wait(barrier, slots_in)

    point_hop = hop(prow.at[pl.ds(0, REACH)], prow.at[pl.ds(half, REACH)], 0, before, twin)
    rim_hop = hop(own.at[pl.ds(0, REACH)], d.at[mine, pl.ds(half, REACH)], 1, before, even + 1, 1 + mine)
    rim_in = [
        hop(own.at[pl.ds(0, REACH)], d.at[k, pl.ds(half, REACH)], 1, before, even + 1, 1 + k)
        for k in range(2)
    ]
    twin_hop = hop(own.at[pl.ds(twin_base, half)], d.at[mine, pl.ds(0, half)], 3, me, twin)
    ring_hop = hop(own.at[pl.ds(half, REACH)], d.at[mine, pl.ds(half, REACH)], 4, me, twin)
    twin_hop.start()

    @pl.when(mine == 1)
    def _():
        ring_hop.start()

    @pl.when(jnp.logical_and(mine == 0, me > 0))
    def _():
        point_hop.start()

    @pl.when(me > 0)
    def _():
        rim_hop.start()

    for k in range(half):
        d[mine, k] = own[base + k]

    @pl.when(mine == 0)
    def _():
        for k in range(half, span):
            d[0, k] = own[k]

    @pl.when(jnp.logical_and(mine == 1, me == n - 1))
    def _():
        d[:, pl.ds(half, REACH)] = jnp.zeros((2, REACH, cols, width), F32)
        prow[pl.ds(half, REACH)] = jnp.zeros((REACH, 8, width), F32)

    twin_hop.wait_recv()
    for k in range(half):
        stack(k, both(d, k))

    low_hop = hop(acc.at[:, pl.ds(0, REACH)], in_high, 5, low_leaf, twin)
    high_hop = hop(acc.at[:, pl.ds(half, REACH)], in_low, 6, high_leaf, twin)

    def first_pass(i, carry):
        @pl.when(jnp.logical_and(i == half - REACH, jnp.logical_and(mine == 1, me < n - 1)))
        def _():
            point_hop.wait_recv()

        @pl.when(i == half - REACH + 1)
        def _():
            @pl.when(mine == 0)
            def _():
                ring_hop.wait_recv()

            @pl.when(jnp.logical_and(mine == 1, me < n - 1))
            def _():
                for k in range(2):
                    rim_in[k].wait_recv()

            for k in range(half, span):
                stack(k, both(d, k))

        build(i)
        products(i - 1, acc)

        @pl.when(jnp.logical_and(i == REACH, has_low))
        def _():
            low_hop.start()

        return carry

    lax.fori_loop(1, half, first_pass, 0)
    products(half - 1, acc)

    @pl.when(has_high)
    def _():
        high_hop.start()

    @pl.when(jnp.logical_not(has_low))
    def _():
        in_low[...] = jnp.zeros_like(in_low)

    @pl.when(jnp.logical_not(has_high))
    def _():
        in_high[...] = jnp.zeros_like(in_high)

    def make_w(k, more):
        xs = []
        for r in range(2):
            x = acc[r, k]
            if more is not None:
                x = x + more[r]
            x = NORM * x - d[r, k]
            w[r, k] = x
            xs.append(x)
        stack(k, jnp.concatenate(xs, axis=0))

    for k in range(REACH, half):
        make_w(k, None)

    @pl.when(has_high)
    def _():
        low_hop.wait_recv()

    for k in range(half, span):
        make_w(k, [in_high[r, k - half] for r in range(2)])

    @pl.when(has_low)
    def _():
        high_hop.wait_recv()

    for k in range(REACH):
        make_w(k, [in_low[r, k] for r in range(2)])

    far_hop = hop(w.at[other, pl.ds(0, half)], wfar, 7, me, twin)
    far_hop.start()

    def second_pass(i, carry):
        products(i, acc2)
        return carry

    lax.fori_loop(0, half, second_pass, 0)

    give_hop = hop(acc2.at[other, pl.ds(0, half)], part.at[pl.ds(0, half)], 8, me, twin)
    give_rim = hop(acc2.at[other, pl.ds(half, REACH)], part.at[pl.ds(half, REACH)], 9, me, twin)
    next_even = hop(acc2.at[0, pl.ds(half, REACH)], part.at[pl.ds(half, REACH)], 9, after, even)
    next_odd = hop(acc2.at[1, pl.ds(half, REACH)], back, 10, after, even + 1)
    give_hop.start()

    @pl.when(mine == 0)
    def _():
        give_rim.start()

    @pl.when(jnp.logical_and(mine == 1, me < n - 1))
    def _():
        next_even.start()
        next_odd.start()

    def lanes(x):
        return x[:, :128] + x[:, 128:] if width == 256 else x

    sums = [jnp.zeros((rows, width), F32) for _ in range(4)]
    for k in range(span):
        wk = both(w, k)
        sums[3] = sums[3] + wk * both(acc2, k)
        if k < half:
            dk = both(d, k)
            sums[0] = sums[0] + dk * dk
            sums[1] = sums[1] + dk * wk
            sums[2] = sums[2] + wk * wk
    stacked = jnp.concatenate([lanes(x) for x in sums], axis=0)
    parts = three(stacked, 1)
    total = dot(jnp.full((8, parts.shape[1]), 1.0, BF16), parts, 1, 1)
    sum_out[...] = total[0:1]
    copies = []
    for slot, leaf, row in peers:
        copy = pltpu.make_async_remote_copy(
            src_ref=sum_out, dst_ref=sum_in.at[slot],
            send_sem=ssem.at[slot], recv_sem=rsem.at[slot],
            device_id={"leaf": leaf, "probe": row}, device_id_type=MESH,
        )
        copy.start()
        copies.append(copy)

    @pl.when(jnp.logical_and(mine == 0, me == 0))
    def _():
        part[pl.ds(half, REACH)] = jnp.zeros((REACH, cols, width), F32)

    @pl.when(jnp.logical_and(mine == 1, me == 0))
    def _():
        back[...] = jnp.zeros_like(back)

    @pl.when(mine == 0)
    def _():
        back[...] = acc2[0, pl.ds(half, REACH)]

    total = sum_out[...]
    for slot, copy in enumerate(copies):
        copy.wait_recv()
        total = total + sum_in[slot]
    seat = lax.broadcasted_iota(jnp.int32, (cols, 128), 1)
    line = lax.broadcasted_iota(jnp.int32, (cols, 128), 0) + mine * cols
    rr, dw, ww, wk = [
        jnp.sum(jnp.where(seat == line + q * rows, total, 0.0), axis=1, keepdims=True)
        for q in range(4)
    ]
    wz = NORM * wk - ww
    m = dw / rr
    alpha0 = rr / (SHIFT * rr + dw)
    uu = ww - m * dw
    tilt = alpha0 * uu / rr
    alpha1 = uu / (SHIFT * uu + (m * (m * dw - 2.0 * ww) + wz) - tilt * uu)
    e = alpha0 * (m + tilt)
    both_alpha = alpha0 * alpha1
    sol_d = alpha0 + alpha1 * e
    res_d = alpha0 * m - SHIFT * alpha1 * e
    res_w = -(alpha0 + alpha1 * e - SHIFT * both_alpha) - both_alpha
    res_z = both_alpha * NORM

    far_hop.wait_recv()
    give_hop.wait_recv()

    @pl.when(mine == 1)
    def _():
        give_rim.wait_recv()

    @pl.when(jnp.logical_and(mine == 0, me > 0))
    def _():
        next_even.wait_recv()

    @pl.when(jnp.logical_and(mine == 1, me > 0))
    def _():
        next_odd.wait_recv()

    def finish(l, dl, wl, zl):
        at = pl.ds(pl.multiple_of(l * width, width), width)
        sol_ref[:, at] = sol_d * dl - both_alpha * wl
        res_ref[:, at] = res_d * dl + res_w * wl + res_z * zl

    for k in range(half):
        near = acc2[mine, k]
        far = part[k]
        if k < REACH:
            near = near + part[half + k]
            far = far + back[k]
        finish(base + k, d[mine, k], w[mine, k], near)
        finish(twin_base + k, own[twin_base + k], wfar[k], far)

    for copy in copies:
        copy.wait_send()
    for copy in (twin_hop, far_hop, give_hop):
        copy.wait_send()

    @pl.when(mine == 1)
    def _():
        ring_hop.wait_send()

    @pl.when(mine == 0)
    def _():
        give_rim.wait_send()

    @pl.when(jnp.logical_and(mine == 0, me > 0))
    def _():
        point_hop.wait_send()

    @pl.when(me > 0)
    def _():
        rim_hop.wait_send()

    @pl.when(has_low)
    def _():
        low_hop.wait_send()

    @pl.when(has_high)
    def _():
        high_hop.wait_send()

    @pl.when(jnp.logical_and(mine == 1, me < n - 1))
    def _():
        next_even.wait_send()
        next_odd.wait_send()


def body(coords, site_order, leaf_pairs, pair_count, probes):
    n = lax.axis_size("leaf")
    leaf_dev, width = site_order.shape
    cols = probes.shape[0]
    half = leaf_dev // 2
    span = half + REACH
    slots_in = 2 * n - 1
    hbm = pl.BlockSpec(memory_space=pl.ANY)
    vmem = pl.BlockSpec(memory_space=pltpu.VMEM)
    field = functools.partial(pltpu.VMEM, dtype=F32)
    return pl.pallas_call(
        functools.partial(kernel, n),
        out_shape=(jax.ShapeDtypeStruct(probes.shape, F32),) * 2,
        in_specs=[hbm] * 5,
        out_specs=(vmem, vmem),
        scratch_shapes=[
            field(coords.shape),
            pltpu.VMEM(site_order.shape, jnp.int32),
            pltpu.VMEM(leaf_pairs.shape, jnp.int32),
            pltpu.SMEM(pair_count.shape, jnp.int32),
            field((leaf_dev, cols, width)),
            field((8, leaf_dev * width)),
            field((span, 8, width)),
            field((3, width, 128)),
            field((half * OFFS, 128)),
            pltpu.VMEM((half * OFFS, 2, width, width), BF16),
            field((2, span, cols, width)),
            field((2, span, cols, width)),
            field((half, cols, width)),
            pltpu.VMEM((span, 4 * cols, width), BF16),
            field((2, span, cols, width)),
            field((2, span, cols, width)),
            field((2, REACH, cols, width)),
            field((2, REACH, cols, width)),
            field((span, cols, width)),
            field((REACH, cols, width)),
            field((1, 128)),
            field((slots_in, 1, 128)),
            pltpu.SemaphoreType.DMA((4 + leaf_dev,)),
            pltpu.SemaphoreType.DMA((slots_in,)),
            pltpu.SemaphoreType.DMA((slots_in,)),
            pltpu.SemaphoreType.DMA((11,)),
            pltpu.SemaphoreType.DMA((11,)),
        ],
        compiler_params=pltpu.CompilerParams(
            collective_id=0, has_side_effects=True, vmem_limit_bytes=48 * 2**20
        ),
    )(coords, site_order, leaf_pairs, pair_count, probes)


def solution(mesh):
    in_specs = (P(None, "leaf"), P("leaf", None), P(None, "leaf"), P("leaf"), P("probe", "leaf"))
    out_specs = (P("probe", "leaf"), P("probe", "leaf"))
    return jax.shard_map(body, mesh=mesh, in_specs=in_specs, out_specs=out_specs, check_vma=False)
```

time: 48.7 us -> 45.5 us (0.934)
  Pallas kernels: 43.2 us -> 40 us
    pallas_call x1, Pallas kernels: 43.2 us -> 40 us  [body(): pl.pallas_call(functools.partial(kernel, n), out_shape=(jax.ShapeDtypeStr...]
where the time goes in v1:
time: 45.5 us; the launch traced here: 45.3 us
  Pallas kernels  40 us (88%)
  local copies, waits for them, and re-layouts  3.92 us (9%)
  between operations  1.32 us (3%)
    pallas_call x1, Pallas kernels, body(): pl.pallas_call(functools.partial(kernel, n), out_shape=(jax.ShapeDtypeStr...  40 us
    unnamed x10, local copies, waits for them, and re-layouts  3.92 us

profile of v1, /device:TPU:0, one launch (start us, length us, event | category | flops | bytes accessed | tf_op | source)
XLA Modules:
  0.0 45.3 jit_solution(7275537080975378642)
XLA Ops:
  0.6 0.0 copy-start.3
  1.3 0.0 copy-done.3
  1.3 0.0 copy-start
  1.3 0.9 %copy-done = f32[16,4096]{1,0:T(8,128)S(1)} copy-done((f32[16,4096]{1,0:T(8,128)S(1)}, f32[16,4096]{1,0:T(8,128)}, u32[]{:S(2)}) %copy-start) | copy-done | bytes 262168
  2.3 0.0 copy-start.1
  2.3 0.8 %copy-done.1 = f32[3,4096]{1,0:T(4,128)S(1)} copy-done((f32[3,4096]{1,0:T(4,128)S(1)}, f32[3,4096]{1,0:T(4,128)}, u32[]{:S(2)}) %copy-start.1) | copy-done | bytes 49176
  3.1 0.0 copy-start.2
  3.1 0.7 %copy-done.2 = s32[16,256]{1,0:T(8,128)S(1)} copy-done((s32[16,256]{1,0:T(8,128)S(1)}, s32[16,256]{1,0:T(8,128)}, u32[]{:S(2)}) %copy-start.2) | copy-done | bytes 16408
  3.8 40.0 %shard_map.68 = (f32[16,4096]{1,0:T(8,128)S(1)}, f32[16,4096]{1,0:T(8,128)S(1)}) custom-call(f32[3,4096]{1,0:T(4,128)S(1)} %copy-done.1, s32[16,256]{1,0:T(8,128)S(1)} %copy-done.2, s32[2,96]{1,0:T(2,128)S(1)} %copy-done.3, s32[1]{0:T(128)S(6)} %copy.9.count_hbm, f32[16,4096]{1,0:T(8,128)S(1)} %copy-done), custom_call_target="tpu_custom_call" | custom-call | tf_op jit(solution)/shard_map/pallas_call | solution.py:463
  43.9 0.7 %copy.10 = f32[16,4096]{1,0:T(8,128)} copy(f32[16,4096]{1,0:T(8,128)S(1)} %get-tuple-element.4) | data formatting | bytes 524288
  44.6 0.7 %copy.11 = f32[16,4096]{1,0:T(8,128)} copy(f32[16,4096]{1,0:T(8,128)S(1)} %get-tuple-element.5) | data formatting | bytes 524288
Async XLA Ops:
  0.6 0.7 %copy-start.3 = (s32[2,96]{1,0:T(2,128)S(1)}, s32[2,96]{1,0:T(2,128)}, u32[]{:S(2)}) copy-start(s32[2,96]{1,0:T(2,128)} %pairs_hbm.1) | copy-start | bytes 2308
  1.3 0.9 %copy-start = (f32[16,4096]{1,0:T(8,128)S(1)}, f32[16,4096]{1,0:T(8,128)}, u32[]{:S(2)}) copy-start(f32[16,4096]{1,0:T(8,128)} %probes_hbm.1) | copy-start | bytes 786436
  2.3 0.8 %copy-start.1 = (f32[3,4096]{1,0:T(4,128)S(1)}, f32[3,4096]{1,0:T(4,128)}, u32[]{:S(2)}) copy-start(f32[3,4096]{1,0:T(4,128)} %coords_hbm.1) | copy-start | bytes 147460
  3.1 0.7 %copy-start.2 = (s32[16,256]{1,0:T(8,128)S(1)}, s32[16,256]{1,0:T(8,128)}, u32[]{:S(2)}) copy-start(s32[16,256]{1,0:T(8,128)} %order_hbm.1) | copy-start | bytes 49156

commit v2 on v1

--- a/solution.py
+++ b/solution.py
@@ -38,9 +38,9 @@
 
 
 def kernel(
-    n, coords_hbm, order_hbm, pairs_hbm, count_hbm, probes_hbm, sol_ref, res_ref,
-    cin, order, pairs, count, own, c8, prow, pcb, mask, tiles, d, w, wfar, v2, acc, acc2,
-    in_low, in_high, part, back, sum_out, sum_in, isem, ssem, rsem, hsend, hrecv,
+    n, coords_hbm, order_hbm, pairs_hbm, probes_hbm, sol_ref, res_ref,
+    cin, order, pairs, own, c8, prow, pcb, mask, tiles, d, w, wfar, v2, acc, acc2,
+    in_low, in_high, part, back, diag, sum_out, sum_in, isem, ssem, rsem, hsend, hrecv,
 ):
     leaf_dev, width = order.shape
     cols = probes_hbm.shape[0]
@@ -70,10 +70,9 @@
 
     loads = [
         load(coords_hbm, cin, 0), load(order_hbm, order, 1), load(pairs_hbm, pairs, 2),
-        load(count_hbm, count, 3),
     ]
     for l in range(leaf_dev):
-        loads.append(load(probes_hbm.at[:, l * width : (l + 1) * width], own.at[l], 4 + l))
+        loads.append(load(probes_hbm.at[:, l * width : (l + 1) * width], own.at[l], 3 + l))
     for copy in loads:
         copy.start()
     barrier = pltpu.get_barrier_semaphore()
@@ -89,102 +88,7 @@
             device_id={"leaf": leaf, "probe": row}, device_id_type=MESH,
         )
 
-    place = lax.broadcasted_iota(jnp.int32, (width, width), 0)
-    for copy in loads[:4]:
-        copy.wait()
-    c8[...] = jnp.zeros_like(c8)
-    c8[0:3, :] = cin[...] * (RATE / TAPER)
-
-    def gather(k):
-        x = c8[:, pl.ds(pl.multiple_of((base + k) * width, width), width)]
-        parts = three(x, 0)
-        onehot = jnp.where(place == order[pl.ds(base + k, 1), :], 1.0, 0.0).astype(BF16)
-        got = dot(parts, onehot, 1, 0)
-        prow[k] = got[0:8] + got[8:16] + got[16:24]
-
-    for k in range(half):
-        gather(k)
-
-    @pl.when(mine == 0)
-    def _():
-        for k in range(half, span):
-            gather(k)
-
-    slots = pairs.shape[1]
-    first = pairs[0:1, :]
-    second = pairs[1:2, :]
-    code = (first - me * leaf_dev - base) * OFFS + (second - first)
-    lane = lax.broadcasted_iota(jnp.int32, (1, slots), 1)
-    code = jnp.where(lane < count[0], code, -1)
-    want = lax.broadcasted_iota(jnp.int32, (half * OFFS, slots), 0)
-    hit = jnp.max(jnp.where(want == code, RATE, 0.0), axis=1, keepdims=True)
-    mask[...] = jnp.broadcast_to(hit, mask.shape)
-    acc[...] = jnp.zeros_like(acc)
-    acc2[...] = jnp.zeros_like(acc2)
-
-    def both(field, k):
-        return jnp.concatenate([field[0, k], field[1, k]], axis=0)
-
-    def stack(k, x):
-        hi = x.astype(BF16)
-        v2[k] = jnp.concatenate([hi, (x - hi.astype(F32)).astype(BF16)], axis=0)
-
-    def add(into, k, x):
-        into[0, k] += x[:cols]
-        into[1, k] += x[cols:]
-
-    rows = 2 * cols
-
-    def products(i, into):
-        vi = v2[i]
-        row = jnp.zeros((2 * rows, width), F32)
-        low = jnp.zeros((rows, width), F32)
-        for o in range(OFFS):
-            hi = tiles[i * OFFS + o, 0]
-            lo = tiles[i * OFFS + o, 1]
-            vj = v2[i + o]
-            row = row + dot(vj, hi, 1, 1)
-            low = low + dot(vj[:rows], lo, 1, 1)
-            if o > 0:
-                col = dot(vi, hi, 1, 0)
-                add(into, i + o, col[:rows] + col[rows:] + dot(vi[:rows], lo, 1, 0))
-        add(into, i, row[:rows] + row[rows:] + low)
-
-    def build(i):
-        turned = prow[i].T
-        for c in range(3):
-            pcb[c] = jnp.broadcast_to(turned[:, c : c + 1], (width, 128))
-        for o in range(OFFS):
-            s = i * OFFS + o
-            for h in range(0, width, 128):
-                listed = mask[pl.ds(s, 1), :]
-                right = [
-                    jnp.broadcast_to(
-                        jnp.where(
-                            listed > 0.0,
-                            prow[i + o, c : c + 1, h : h + 128],
-                            prow[i, c : c + 1, h : h + 128],
-                        ),
-                        (ROWS, 128),
-                    )
-                    for c in range(3)
-                ]
-                top = jnp.broadcast_to(listed, (ROWS, 128))
-                for a in range(0, width, ROWS):
-                    dx = pcb[0, a : a + ROWS, :] - right[0]
-                    dy = pcb[1, a : a + ROWS, :] - right[1]
-                    dz = pcb[2, a : a + ROWS, :] - right[2]
-                    d2 = jnp.maximum(dx * dx + dy * dy + dz * dz, 1e-30)
-                    y = jnp.maximum(top - d2 * lax.rsqrt(d2), 0.0)
-                    y2 = y * y
-                    t = (y2 * y2) * (y2 + (LIN * y + CON)) * jnp.exp2(y)
-                    hi = t.astype(BF16)
-                    tiles[s, 0, a : a + ROWS, h : h + 128] = hi
-                    tiles[s, 1, a : a + ROWS, h : h + 128] = (t - hi.astype(F32)).astype(BF16)
-
-    build(0)
-
-    for copy in loads[4:]:
+    for copy in loads[3:]:
         copy.wait()
     pl.semaphore_wait(barrier, slots_in)
 
@@ -202,13 +106,132 @@
     def _():
         ring_hop.start()
 
+    @pl.when(me > 0)
+    def _():
+        rim_hop.start()
+
+    place = lax.broadcasted_iota(jnp.int32, (width, width), 0)
+    for copy in loads[:3]:
+        copy.wait()
+    c8[...] = jnp.zeros_like(c8)
+    c8[0:3, :] = cin[...] * (RATE / TAPER)
+
+    def gather(k):
+        x = c8[:, pl.ds(pl.multiple_of((base + k) * width, width), width)]
+        parts = three(x, 0)
+        onehot = jnp.where(place == order[pl.ds(base + k, 1), :], 1.0, 0.0).astype(BF16)
+        got = dot(parts, onehot, 1, 0)
+        prow[k] = got[0:8] + got[8:16] + got[16:24]
+
+    for k in range(half):
+        gather(k)
+
+    @pl.when(mine == 0)
+    def _():
+        for k in range(half, span):
+            gather(k)
+
+    slots = pairs.shape[1]
+    first = pairs[0:1, :]
+    second = pairs[1:2, :]
+    code = (first - me * leaf_dev - base) * OFFS + (second - first)
+    want = lax.broadcasted_iota(jnp.int32, (half * OFFS, slots), 0)
+    hit = jnp.max(jnp.where(want == code, RATE, 0.0), axis=1, keepdims=True)
+    mask[...] = jnp.broadcast_to(hit, mask.shape)
+    acc[...] = jnp.zeros_like(acc)
+    acc2[...] = jnp.zeros_like(acc2)
+
     @pl.when(jnp.logical_and(mine == 0, me > 0))
     def _():
         point_hop.start()
 
-    @pl.when(me > 0)
-    def _():
-        rim_hop.start()
+    def both(field, k):
+        return jnp.concatenate([field[0, k], field[1, k]], axis=0)
+
+    def stack(k, x):
+        hi = x.astype(BF16)
+        v2[k] = jnp.concatenate([hi, (x - hi.astype(F32)).astype(BF16)], axis=0)
+
+    def add(into, k, x):
+        into[0, k] += x[:cols]
+        into[1, k] += x[cols:]
+
+    rows = 2 * cols
+
+    def tile(s):
+        return [
+            jnp.concatenate([tiles[s, p, h] for h in range(width // 128)], axis=1)
+            for p in range(2)
+        ]
+
+    def columns(vi, hi, lo):
+        x = dot(vi, hi, 1, 0)
+        return x[:rows] + x[rows:] + dot(vi[:rows], lo, 1, 0)
+
+    def products(i, into, make=None):
+        vi = v2[i]
+        row = jnp.zeros((2 * rows, width), F32)
+        low = jnp.zeros((rows, width), F32)
+        for o in range(OFFS):
+            if make is not None:
+                make(i, o)
+            hi, lo = tile(i * OFFS + o)
+            vj = v2[i + o]
+            row = row + dot(vj, hi, 1, 1)
+            low = low + dot(vj[:rows], lo, 1, 1)
+            if o > 0:
+                add(into, i + o, columns(vi, hi, lo))
+        add(into, i, row[:rows] + row[rows:] + low)
+
+    def first_products(i):
+        vi = v2[i]
+        for o in range(OFFS):
+            hi, lo = tile(i * OFFS + o)
+            x = columns(vi, hi, lo)
+            if o > 0:
+                add(acc2, i + o, x)
+            else:
+                diag[i] = x
+
+    def last_products(i):
+        row = jnp.zeros((2 * rows, width), F32)
+        low = jnp.zeros((rows, width), F32)
+        for o in range(1, OFFS):
+            hi, lo = tile(i * OFFS + o)
+            vj = v2[i + o]
+            row = row + dot(vj, hi, 1, 1)
+            low = low + dot(vj[:rows], lo, 1, 1)
+        add(acc2, i, row[:rows] + row[rows:] + low + diag[i])
+
+    def turn(i):
+        turned = prow[i].T
+        for c in range(3):
+            pcb[c] = jnp.broadcast_to(turned[:, c : c + 1], (width, 128))
+
+    def build(i, o):
+        s = i * OFFS + o
+        for h in range(width // 128):
+            at = slice(h * 128, h * 128 + 128)
+            listed = mask[pl.ds(s, 1), :]
+            right = [
+                jnp.broadcast_to(
+                    jnp.where(listed > 0.0, prow[i + o, c : c + 1, at], prow[i, c : c + 1, at]),
+                    (ROWS, 128),
+                )
+                for c in range(3)
+            ]
+            top = jnp.broadcast_to(listed, (ROWS, 128))
+            for a in range(0, width, ROWS):
+                dx = pcb[0, a : a + ROWS, :] - right[0]
+                dy = pcb[1, a : a + ROWS, :] - right[1]
+                dz = pcb[2, a : a + ROWS, :] - right[2]
+                d2 = jnp.maximum(dx * dx + dy * dy + dz * dz, 1e-30)
+                y = jnp.maximum(top - d2 * lax.rsqrt(d2), 0.0)
+                y2 = y * y
+                t = (y2 * y2) * (y2 + (LIN * y + CON)) * jnp.exp2(y)
+                hi = t.astype(BF16)
+                tiles[s, 0, h, a : a + ROWS, :] = hi
+                tiles[s, 1, h, a : a + ROWS, :] = (t - hi.astype(F32)).astype(BF16)
 
     for k in range(half):
         d[mine, k] = own[base + k]
@@ -235,7 +258,7 @@
         def _():
             point_hop.wait_recv()
 
-        @pl.when(i == half - REACH + 1)
+        @pl.when(i == half - REACH)
         def _():
             @pl.when(mine == 0)
             def _():
@@ -249,17 +272,16 @@
             for k in range(half, span):
                 stack(k, both(d, k))
 
-        build(i)
-        products(i - 1, acc)
-
-        @pl.when(jnp.logical_and(i == REACH, has_low))
+        turn(i)
+        products(i, acc, build)
+
+        @pl.when(jnp.logical_and(i == REACH - 1, has_low))
         def _():
             low_hop.start()
 
         return carry
 
-    lax.fori_loop(1, half, first_pass, 0)
-    products(half - 1, acc)
+    lax.fori_loop(0, half, first_pass, 0)
 
     @pl.when(has_high)
     def _():
@@ -294,6 +316,15 @@
     for k in range(half, span):
         make_w(k, [in_high[r, k - half] for r in range(2)])
 
+    def whole_pass(i, carry):
+        products(i, acc2)
+        return carry
+
+    lax.fori_loop(REACH, half, whole_pass, 0)
+    early = jnp.zeros((rows, width), F32)
+    for k in range(REACH, span):
+        early = early + both(w, k) * both(acc2, k)
+
     @pl.when(has_low)
     def _():
         high_hop.wait_recv()
@@ -303,27 +334,27 @@
 
     far_hop = hop(w.at[other, pl.ds(0, half)], wfar, 7, me, twin)
     far_hop.start()
-
-    def second_pass(i, carry):
-        products(i, acc2)
-        return carry
-
-    lax.fori_loop(0, half, second_pass, 0)
-
     give_hop = hop(acc2.at[other, pl.ds(0, half)], part.at[pl.ds(0, half)], 8, me, twin)
     give_rim = hop(acc2.at[other, pl.ds(half, REACH)], part.at[pl.ds(half, REACH)], 9, me, twin)
     next_even = hop(acc2.at[0, pl.ds(half, REACH)], part.at[pl.ds(half, REACH)], 9, after, even)
     next_odd = hop(acc2.at[1, pl.ds(half, REACH)], back, 10, after, even + 1)
-    give_hop.start()
-
-    @pl.when(mine == 0)
-    def _():
-        give_rim.start()
-
-    @pl.when(jnp.logical_and(mine == 1, me < n - 1))
-    def _():
-        next_even.start()
-        next_odd.start()
+
+    def first_half(t, carry):
+        i = REACH - 1 - t
+        first_products(i)
+
+        @pl.when(jnp.logical_and(i == half - REACH, mine == 0))
+        def _():
+            give_rim.start()
+
+        @pl.when(jnp.logical_and(i == half - REACH, jnp.logical_and(mine == 1, me < n - 1)))
+        def _():
+            next_even.start()
+            next_odd.start()
+
+        return carry
+
+    lax.fori_loop(0, REACH, first_half, 0)
 
     def lanes(x):
         return x[:, :128] + x[:, 128:] if width == 256 else x
@@ -332,11 +363,14 @@
     for k in range(span):
         wk = both(w, k)
         sums[3] = sums[3] + wk * both(acc2, k)
+        if k < REACH:
+            early = early - wk * diag[k]
         if k < half:
             dk = both(d, k)
             sums[0] = sums[0] + dk * dk
             sums[1] = sums[1] + dk * wk
             sums[2] = sums[2] + wk * wk
+    sums[3] = 2.0 * sums[3] - early
     stacked = jnp.concatenate([lanes(x) for x in sums], axis=0)
     parts = three(stacked, 1)
     total = dot(jnp.full((8, parts.shape[1]), 1.0, BF16), parts, 1, 1)
@@ -350,6 +384,13 @@
         )
         copy.start()
         copies.append(copy)
+
+    def last_half(i, carry):
+        last_products(i)
+        return carry
+
+    lax.fori_loop(0, REACH, last_half, 0)
+    give_hop.start()
 
     @pl.when(jnp.logical_and(mine == 0, me == 0))
     def _():
@@ -457,25 +498,24 @@
     half = leaf_dev // 2
     span = half + REACH
     slots_in = 2 * n - 1
-    hbm = pl.BlockSpec(memory_space=pl.ANY)
+    hbm = pl.BlockSpec(memory_space=pltpu.HBM)
     vmem = pl.BlockSpec(memory_space=pltpu.VMEM)
     field = functools.partial(pltpu.VMEM, dtype=F32)
     return pl.pallas_call(
         functools.partial(kernel, n),
         out_shape=(jax.ShapeDtypeStruct(probes.shape, F32),) * 2,
-        in_specs=[hbm] * 5,
+        in_specs=[hbm] * 4,
         out_specs=(vmem, vmem),
         scratch_shapes=[
             field(coords.shape),
             pltpu.VMEM(site_order.shape, jnp.int32),
             pltpu.VMEM(leaf_pairs.shape, jnp.int32),
-            pltpu.SMEM(pair_count.shape, jnp.int32),
             field((leaf_dev, cols, width)),
             field((8, leaf_dev * width)),
             field((span, 8, width)),
             field((3, width, 128)),
             field((half * OFFS, 128)),
-            pltpu.VMEM((half * OFFS, 2, width, width), BF16),
+            pltpu.VMEM((half * OFFS, 2, width // 128, width, 128), BF16),
             field((2, span, cols, width)),
             field((2, span, cols, width)),
             field((half, cols, width)),
@@ -486,18 +526,19 @@
             field((2, REACH, cols, width)),
             field((span, cols, width)),
             field((REACH, cols, width)),
+            field((REACH, 2 * cols, width)),
             field((1, 128)),
             field((slots_in, 1, 128)),
-            pltpu.SemaphoreType.DMA((4 + leaf_dev,)),
+            pltpu.SemaphoreType.DMA((3 + leaf_dev,)),
             pltpu.SemaphoreType.DMA((slots_in,)),
             pltpu.SemaphoreType.DMA((slots_in,)),
             pltpu.SemaphoreType.DMA((11,)),
             pltpu.SemaphoreType.DMA((11,)),
         ],
         compiler_params=pltpu.CompilerParams(
-            collective_id=0, has_side_effects=True, vmem_limit_bytes=48 * 2**20
+            collective_id=0, has_side_effects=True, vmem_limit_bytes=67043328
         ),
-    )(coords, site_order, leaf_pairs, pair_count, probes)
+    )(coords, site_order, leaf_pairs, probes)
 
 
 def solution(mesh):

time: 45.5 us -> 35.8 us (0.79)
  Pallas kernels: 40 us -> 32.5 us
  local copies, waits for them, and re-layouts: 3.92 us -> 2.42 us
  between operations: 1.32 us -> 0.65 us
    pallas_call x1, Pallas kernels: 40 us -> 32.5 us  [body(): pl.pallas_call(functools.partial(kernel, n), out_shape=(jax.ShapeDtypeStr...]
    unnamed x10 -> x4, local copies, waits for them, and re-layouts: 3.92 us -> 2.42 us
where the time goes in v2:
time: 35.8 us; the launch traced here: 35.6 us
  Pallas kernels  32.5 us (91%)
  local copies, waits for them, and re-layouts  2.42 us (7%)
  between operations  0.65 us (2%)
    pallas_call x1, Pallas kernels, body(): pl.pallas_call(functools.partial(kernel, n), out_shape=(jax.ShapeDtypeStr...  32.5 us
    unnamed x4, local copies, waits for them, and re-layouts  2.42 us

profile of v2, /device:TPU:0, one launch (start us, length us, event | category | flops | bytes accessed | tf_op | source)
XLA Modules:
  0.0 35.6 jit_solution(15743131123030016298)
XLA Ops:
  0.6 32.5 %shard_map.59 = (f32[16,4096]{1,0:T(8,128)}, f32[16,4096]{1,0:T(8,128)}) custom-call(f32[3,4096]{1,0:T(4,128)} %coords_hbm.1, s32[16,256]{1,0:T(8,128)} %order_hbm.1, s32[2,96]{1,0:T(2,128)} %pairs_hbm.1, f32[16,4096]{1,0:T(8,128)} %probes_hbm.1), custom_call_target="tpu_custom_call" | custom-call | tf_op jit(solution)/shard_map/pallas_call | solution.py:504
  33.2 0.0 copy-start
  33.2 1.7 %copy.8 = f32[16,4096]{1,0:T(8,128)} copy(f32[16,4096]{1,0:T(8,128)} %get-tuple-element.4) | data formatting | bytes 524288
  34.9 0.0 copy-done
  34.9 0.7 %copy.9 = f32[16,4096]{1,0:T(8,128)} copy(f32[16,4096]{1,0:T(8,128)S(1)} %copy-done) | data formatting | bytes 524288
Async XLA Ops:
  33.2 1.7 %copy-start = (f32[16,4096]{1,0:T(8,128)S(1)}, f32[16,4096]{1,0:T(8,128)}, u32[]{:S(2)}) copy-start(f32[16,4096]{1,0:T(8,128)} %get-tuple-element.5) | copy-start | bytes 786436

commit v3 on v2

--- a/solution.py
+++ b/solution.py
@@ -21,6 +21,7 @@
 CON = 5.0 * (1.0 + GROW) * RATE**2 / QUAD
 NORM = QUAD * 2.0**-RATE / RATE**6
 OFFS = REACH + 1
+AHEAD = 1
 ROWS = 32
 MESH = pl.DeviceIdType.MESH
 F32 = jnp.float32
@@ -40,7 +41,7 @@
 def kernel(
     n, coords_hbm, order_hbm, pairs_hbm, probes_hbm, sol_ref, res_ref,
     cin, order, pairs, own, c8, prow, pcb, mask, tiles, d, w, wfar, v2, acc, acc2,
-    in_low, in_high, part, back, diag, sum_out, sum_in, isem, ssem, rsem, hsend, hrecv,
+    in_edge, in_twin, part, back, diag, sum_out, sum_in, word, line_done, isem, ssem, rsem, hsend, hrecv,
 ):
     leaf_dev, width = order.shape
     cols = probes_hbm.shape[0]
@@ -56,10 +57,10 @@
     twin_base = half * other
     after = lax.rem(me + 1, n)
     before = lax.rem(me + n - 1, n)
-    low_leaf = jnp.where(mine == 0, before, me)
-    high_leaf = jnp.where(mine == 0, me, after)
-    has_low = jnp.logical_or(mine == 1, me > 0)
-    has_high = jnp.logical_or(mine == 0, me < n - 1)
+    edge_leaf = jnp.where(mine == 0, before, after)
+    has_edge = jnp.where(mine == 0, me > 0, me < n - 1)
+    edge = half * mine
+    inner = half * other
 
     peers = [(k - 1, lax.rem(me + k, n), probe) for k in range(1, n)]
     peers += [(n - 1 + k, lax.rem(me + k, n), twin) for k in range(n)]
@@ -76,10 +77,44 @@
     for copy in loads:
         copy.start()
     barrier = pltpu.get_barrier_semaphore()
-    for _, leaf, row in peers:
+    def greet(sem, leaf, row):
         pl.semaphore_signal(
-            barrier, inc=1, device_id={"leaf": leaf, "probe": row}, device_id_type=MESH
+            sem, inc=1, device_id={"leaf": leaf, "probe": row}, device_id_type=MESH
         )
+
+    greet(barrier, me, twin)
+
+    @pl.when(me > 0)
+    def _():
+        greet(barrier, me - 1, probe)
+        greet(barrier, me - 1, twin)
+
+    @pl.when(me < n - 1)
+    def _():
+        greet(barrier, me + 1, probe)
+        greet(barrier, me + 1, twin)
+
+    steps = []
+    while (1 << len(steps)) < n - 1:
+        steps.append(1 << len(steps))
+
+    def tell(j):
+        @pl.when(me >= steps[j])
+        def _():
+            greet(word.at[2 * j], me - steps[j], probe)
+
+        @pl.when(me + steps[j] < n)
+        def _():
+            greet(word.at[2 * j + 1], me + steps[j], probe)
+
+    def hear(j):
+        @pl.when(me + steps[j] < n)
+        def _():
+            pl.semaphore_wait(word.at[2 * j], 1)
+
+        @pl.when(me >= steps[j])
+        def _():
+            pl.semaphore_wait(word.at[2 * j + 1], 1)
 
     def hop(src, dst, slot, leaf, row, landing=None):
         return pltpu.make_async_remote_copy(
@@ -90,7 +125,9 @@
 
     for copy in loads[3:]:
         copy.wait()
-    pl.semaphore_wait(barrier, slots_in)
+    near = jnp.where(me > 0, 2, 0) + jnp.where(me < n - 1, 2, 0)
+    pl.semaphore_wait(barrier, 1 + near)
+    tell(0)
 
     point_hop = hop(prow.at[pl.ds(0, REACH)], prow.at[pl.ds(half, REACH)], 0, before, twin)
     rim_hop = hop(own.at[pl.ds(0, REACH)], d.at[mine, pl.ds(half, REACH)], 1, before, even + 1, 1 + mine)
@@ -168,20 +205,21 @@
         x = dot(vi, hi, 1, 0)
         return x[:rows] + x[rows:] + dot(vi[:rows], lo, 1, 0)
 
-    def products(i, into, make=None):
+    def products(i, into, make):
         vi = v2[i]
-        row = jnp.zeros((2 * rows, width), F32)
-        low = jnp.zeros((rows, width), F32)
+        cut = width // 2
+        row = [jnp.zeros((cut, 2 * rows), F32) for _ in range(2)]
         for o in range(OFFS):
-            if make is not None:
-                make(i, o)
+            make(i, o)
             hi, lo = tile(i * OFFS + o)
             vj = v2[i + o]
-            row = row + dot(vj, hi, 1, 1)
-            low = low + dot(vj[:rows], lo, 1, 1)
+            for q in range(2):
+                at = slice(q * cut, q * cut + cut)
+                row[q] = row[q] + dot(hi[at], vj, 1, 1) + dot(lo[at], vj, 1, 1)
             if o > 0:
                 add(into, i + o, columns(vi, hi, lo))
-        add(into, i, row[:rows] + row[rows:] + low)
+        row = jnp.concatenate([x.T for x in row], axis=1)
+        add(into, i, row[:rows] + row[rows:])
 
     def first_products(i):
         vi = v2[i]
@@ -250,15 +288,16 @@
     for k in range(half):
         stack(k, both(d, k))
 
-    low_hop = hop(acc.at[:, pl.ds(0, REACH)], in_high, 5, low_leaf, twin)
-    high_hop = hop(acc.at[:, pl.ds(half, REACH)], in_low, 6, high_leaf, twin)
-
-    def first_pass(i, carry):
-        @pl.when(jnp.logical_and(i == half - REACH, jnp.logical_and(mine == 1, me < n - 1)))
-        def _():
-            point_hop.wait_recv()
-
-        @pl.when(i == half - REACH)
+    edge_hop = hop(acc.at[:, pl.ds(edge, REACH)], in_edge, 5, edge_leaf, twin)
+    inner_hop = hop(acc.at[:, pl.ds(inner, REACH)], in_twin, 6, me, twin)
+    lag = half - REACH
+
+    def first_pass(t, carry):
+        i = jnp.where(
+            mine == 0, t, jnp.where(t < AHEAD, t, jnp.where(t < AHEAD + REACH, t + lag - AHEAD, t - REACH))
+        )
+
+        @pl.when(i == lag)
         def _():
             @pl.when(mine == 0)
             def _():
@@ -266,34 +305,37 @@
 
             @pl.when(jnp.logical_and(mine == 1, me < n - 1))
             def _():
+                point_hop.wait_recv()
                 for k in range(2):
                     rim_in[k].wait_recv()
 
             for k in range(half, span):
                 stack(k, both(d, k))
 
+        for j in range(len(steps) - 1):
+            @pl.when(t == 2 * j + 1)
+            def _(j=j):
+                hear(j)
+                tell(j + 1)
+
         turn(i)
         products(i, acc, build)
 
-        @pl.when(jnp.logical_and(i == REACH - 1, has_low))
-        def _():
-            low_hop.start()
+        @pl.when(jnp.logical_and(t == REACH - 1 + AHEAD * mine, has_edge))
+        def _():
+            edge_hop.start()
 
         return carry
 
     lax.fori_loop(0, half, first_pass, 0)
-
-    @pl.when(has_high)
-    def _():
-        high_hop.start()
-
-    @pl.when(jnp.logical_not(has_low))
-    def _():
-        in_low[...] = jnp.zeros_like(in_low)
-
-    @pl.when(jnp.logical_not(has_high))
-    def _():
-        in_high[...] = jnp.zeros_like(in_high)
+    inner_hop.start()
+    for j in range(half // 2, len(steps) - 1):
+        hear(j)
+        tell(j + 1)
+
+    @pl.when(jnp.logical_not(has_edge))
+    def _():
+        in_edge[...] = jnp.zeros_like(in_edge)
 
     def make_w(k, more):
         xs = []
@@ -309,28 +351,21 @@
     for k in range(REACH, half):
         make_w(k, None)
 
-    @pl.when(has_high)
-    def _():
-        low_hop.wait_recv()
-
-    for k in range(half, span):
-        make_w(k, [in_high[r, k - half] for r in range(2)])
-
-    def whole_pass(i, carry):
-        products(i, acc2)
+    @pl.when(has_edge)
+    def _():
+        edge_hop.wait_recv()
+
+    for k in range(REACH):
+        make_w(edge + k, [in_edge[r, k] for r in range(2)])
+
+    def outer_columns(t, carry):
+        first_products(t + REACH * mine)
         return carry
 
-    lax.fori_loop(REACH, half, whole_pass, 0)
-    early = jnp.zeros((rows, width), F32)
-    for k in range(REACH, span):
-        early = early + both(w, k) * both(acc2, k)
-
-    @pl.when(has_low)
-    def _():
-        high_hop.wait_recv()
-
+    lax.fori_loop(0, lag, outer_columns, 0)
+    inner_hop.wait_recv()
     for k in range(REACH):
-        make_w(k, [in_low[r, k] for r in range(2)])
+        make_w(inner + k, [in_twin[r, k] for r in range(2)])
 
     far_hop = hop(w.at[other, pl.ds(0, half)], wfar, 7, me, twin)
     far_hop.start()
@@ -339,15 +374,17 @@
     next_even = hop(acc2.at[0, pl.ds(half, REACH)], part.at[pl.ds(half, REACH)], 9, after, even)
     next_odd = hop(acc2.at[1, pl.ds(half, REACH)], back, 10, after, even + 1)
 
+    left = lag * other
+
     def first_half(t, carry):
-        i = REACH - 1 - t
+        i = left + REACH - 1 - t
         first_products(i)
 
-        @pl.when(jnp.logical_and(i == half - REACH, mine == 0))
+        @pl.when(jnp.logical_and(i == lag, mine == 0))
         def _():
             give_rim.start()
 
-        @pl.when(jnp.logical_and(i == half - REACH, jnp.logical_and(mine == 1, me < n - 1)))
+        @pl.when(jnp.logical_and(i == lag, jnp.logical_and(mine == 1, me < n - 1)))
         def _():
             next_even.start()
             next_odd.start()
@@ -360,21 +397,25 @@
         return x[:, :128] + x[:, 128:] if width == 256 else x
 
     sums = [jnp.zeros((rows, width), F32) for _ in range(4)]
+    own_part = jnp.zeros((rows, width), F32)
     for k in range(span):
         wk = both(w, k)
         sums[3] = sums[3] + wk * both(acc2, k)
-        if k < REACH:
-            early = early - wk * diag[k]
+        if k < half:
+            own_part = own_part + wk * diag[k]
         if k < half:
             dk = both(d, k)
             sums[0] = sums[0] + dk * dk
             sums[1] = sums[1] + dk * wk
             sums[2] = sums[2] + wk * wk
-    sums[3] = 2.0 * sums[3] - early
+    sums[3] = 2.0 * sums[3] + own_part
     stacked = jnp.concatenate([lanes(x) for x in sums], axis=0)
     parts = three(stacked, 1)
     total = dot(jnp.full((8, parts.shape[1]), 1.0, BF16), parts, 1, 1)
     sum_out[...] = total[0:1]
+    hear(len(steps) - 1)
+    greet(line_done, me, twin)
+    pl.semaphore_wait(line_done, 1)
     copies = []
     for slot, leaf, row in peers:
         copy = pltpu.make_async_remote_copy(
@@ -389,7 +430,7 @@
         last_products(i)
         return carry
 
-    lax.fori_loop(0, REACH, last_half, 0)
+    lax.fori_loop(0, half, last_half, 0)
     give_hop.start()
 
     @pl.when(jnp.logical_and(mine == 0, me == 0))
@@ -458,7 +499,7 @@
 
     for copy in copies:
         copy.wait_send()
-    for copy in (twin_hop, far_hop, give_hop):
+    for copy in (twin_hop, inner_hop, far_hop, give_hop):
         copy.wait_send()
 
     @pl.when(mine == 1)
@@ -477,13 +518,9 @@
     def _():
         rim_hop.wait_send()
 
-    @pl.when(has_low)
-    def _():
-        low_hop.wait_send()
-
-    @pl.when(has_high)
-    def _():
-        high_hop.wait_send()
+    @pl.when(has_edge)
+    def _():
+        edge_hop.wait_send()
 
     @pl.when(jnp.logical_and(mine == 1, me < n - 1))
     def _():
@@ -492,6 +529,7 @@
 
 
 def body(coords, site_order, leaf_pairs, pair_count, probes):
+    arrays = (coords, site_order, leaf_pairs, probes)
     n = lax.axis_size("leaf")
     leaf_dev, width = site_order.shape
     cols = probes.shape[0]
@@ -526,9 +564,11 @@
             field((2, REACH, cols, width)),
             field((span, cols, width)),
             field((REACH, cols, width)),
-            field((REACH, 2 * cols, width)),
+            field((half, 2 * cols, width)),
             field((1, 128)),
             field((slots_in, 1, 128)),
+            pltpu.SemaphoreType.REGULAR((2 * n.bit_length(),)),
+            pltpu.SemaphoreType.REGULAR,
             pltpu.SemaphoreType.DMA((3 + leaf_dev,)),
             pltpu.SemaphoreType.DMA((slots_in,)),
             pltpu.SemaphoreType.DMA((slots_in,)),
@@ -536,9 +576,9 @@
             pltpu.SemaphoreType.DMA((11,)),
         ],
         compiler_params=pltpu.CompilerParams(
-            collective_id=0, has_side_effects=True, vmem_limit_bytes=67043328
+            collective_id=0, has_side_effects=True, vmem_limit_bytes=48 * 2**20
         ),
-    )(coords, site_order, leaf_pairs, probes)
+    )(*[pltpu.with_memory_space_constraint(x, pltpu.HBM) for x in arrays])
 
 
 def solution(mesh):

time: 35.8 us -> 32.2 us (0.90)
  Pallas kernels: 32.5 us -> 30 us
  local copies, waits for them, and re-layouts: 2.42 us -> 1.41 us
    pallas_call x1, Pallas kernels: 32.5 us -> 30 us  [body(): pl.pallas_call(functools.partial(kernel, n), out_shape=(jax.ShapeDtypeStr...]
    unnamed x4 -> x2, local copies, waits for them, and re-layouts: 2.42 us -> 1.41 us
where the time goes in v3:
time: 32.2 us; the launch traced here: 32.1 us
  Pallas kernels  30 us (93%)
  local copies, waits for them, and re-layouts  1.41 us (4%)
  between operations  0.64 us (2%)
    pallas_call x1, Pallas kernels, body(): pl.pallas_call(functools.partial(kernel, n), out_shape=(jax.ShapeDtypeStr...  30 us
    unnamed x2, local copies, waits for them, and re-layouts  1.41 us

profile of v3, /device:TPU:0, one launch (start us, length us, event | category | flops | bytes accessed | tf_op | source)
XLA Modules:
  0.0 32.1 jit_solution(10282875471224569297)
XLA Ops:
  0.6 30.0 %shard_map.59 = (f32[16,4096]{1,0:T(8,128)S(1)}, f32[16,4096]{1,0:T(8,128)S(1)}) custom-call(f32[3,4096]{1,0:T(4,128)} %coords_hbm.1, s32[16,256]{1,0:T(8,128)} %order_hbm.1, s32[2,96]{1,0:T(2,128)} %pairs_hbm.1, f32[16,4096]{1,0:T(8,128)} %probes_hbm.1), custom_call_target="tpu_custom_call" | custom-call | tf_op jit(solution)/shard_map/pallas_call | solution.py:542
  30.7 0.7 %copy.8 = f32[16,4096]{1,0:T(8,128)} copy(f32[16,4096]{1,0:T(8,128)S(1)} %get-tuple-element.4) | data formatting | bytes 524288
  31.4 0.7 %copy.9 = f32[16,4096]{1,0:T(8,128)} copy(f32[16,4096]{1,0:T(8,128)S(1)} %get-tuple-element.5) | data formatting | bytes 524288

commit v4 on v3

--- a/solution.py
+++ b/solution.py
@@ -39,9 +39,9 @@
 
 
 def kernel(
-    n, coords_hbm, order_hbm, pairs_hbm, probes_hbm, sol_ref, res_ref,
+    n, coords_hbm, order_hbm, pairs_hbm, probes_hbm, out_ref,
     cin, order, pairs, own, c8, prow, pcb, mask, tiles, d, w, wfar, v2, acc, acc2,
-    in_edge, in_twin, part, back, diag, sum_out, sum_in, word, line_done, isem, ssem, rsem, hsend, hrecv,
+    in_edge, in_twin, part, back, diag, sum_out, sum_in, word, line_done, isem, ssem, rsem, hsend, hrecv, esend, erecv,
 ):
     leaf_dev, width = order.shape
     cols = probes_hbm.shape[0]
@@ -72,10 +72,22 @@
     loads = [
         load(coords_hbm, cin, 0), load(order_hbm, order, 1), load(pairs_hbm, pairs, 2),
     ]
-    for l in range(leaf_dev):
-        loads.append(load(probes_hbm.at[:, l * width : (l + 1) * width], own.at[l], 3 + l))
+    def leaves(ref, first, count):
+        return ref.at[:, pl.ds(pl.multiple_of(first * width, width), count * width)]
+
+    def into_d(r, first, count):
+        return d.at[r, :, first * width : (first + count) * width]
+
+    loads.append(load(leaves(probes_hbm, base, half), into_d(mine, 0, half), 3))
+    loads.append(load(leaves(probes_hbm, twin_base, half), own, 4))
+    ring_load = load(leaves(probes_hbm, half, REACH), into_d(0, half, REACH), 5)
     for copy in loads:
         copy.start()
+
+    @pl.when(mine == 0)
+    def _():
+        ring_load.start()
+
     barrier = pltpu.get_barrier_semaphore()
     def greet(sem, leaf, row):
         pl.semaphore_signal(
@@ -84,37 +96,36 @@
 
     greet(barrier, me, twin)
 
-    @pl.when(me > 0)
-    def _():
-        greet(barrier, me - 1, probe)
-        greet(barrier, me - 1, twin)
-
     @pl.when(me < n - 1)
     def _():
         greet(barrier, me + 1, probe)
         greet(barrier, me + 1, twin)
 
-    steps = []
-    while (1 << len(steps)) < n - 1:
-        steps.append(1 << len(steps))
+    steps = [1]
+    while (1 << len(steps) - 1) < n - 1:
+        steps.append(1 << len(steps) - 1)
 
     def tell(j):
         @pl.when(me >= steps[j])
         def _():
             greet(word.at[2 * j], me - steps[j], probe)
 
-        @pl.when(me + steps[j] < n)
-        def _():
-            greet(word.at[2 * j + 1], me + steps[j], probe)
+        if j > 0:
+
+            @pl.when(me + steps[j] < n)
+            def _():
+                greet(word.at[2 * j + 1], me + steps[j], probe)
 
     def hear(j):
         @pl.when(me + steps[j] < n)
         def _():
             pl.semaphore_wait(word.at[2 * j], 1)
 
-        @pl.when(me >= steps[j])
-        def _():
-            pl.semaphore_wait(word.at[2 * j + 1], 1)
+        if j > 0:
+
+            @pl.when(me >= steps[j])
+            def _():
+                pl.semaphore_wait(word.at[2 * j + 1], 1)
 
     def hop(src, dst, slot, leaf, row, landing=None):
         return pltpu.make_async_remote_copy(
@@ -123,20 +134,17 @@
             device_id={"leaf": leaf, "probe": row}, device_id_type=MESH,
         )
 
-    for copy in loads[3:]:
-        copy.wait()
-    near = jnp.where(me > 0, 2, 0) + jnp.where(me < n - 1, 2, 0)
-    pl.semaphore_wait(barrier, 1 + near)
+    pl.semaphore_wait(barrier, 1 + jnp.where(me > 0, 2, 0))
     tell(0)
 
     point_hop = hop(prow.at[pl.ds(0, REACH)], prow.at[pl.ds(half, REACH)], 0, before, twin)
-    rim_hop = hop(own.at[pl.ds(0, REACH)], d.at[mine, pl.ds(half, REACH)], 1, before, even + 1, 1 + mine)
+    rim_hop = hop(leaves(probes_hbm, 0, REACH), into_d(mine, half, REACH), 1, before, even + 1, 1 + mine)
     rim_in = [
-        hop(own.at[pl.ds(0, REACH)], d.at[k, pl.ds(half, REACH)], 1, before, even + 1, 1 + k)
+        hop(leaves(probes_hbm, 0, REACH), into_d(k, half, REACH), 1, before, even + 1, 1 + k)
         for k in range(2)
     ]
-    twin_hop = hop(own.at[pl.ds(twin_base, half)], d.at[mine, pl.ds(0, half)], 3, me, twin)
-    ring_hop = hop(own.at[pl.ds(half, REACH)], d.at[mine, pl.ds(half, REACH)], 4, me, twin)
+    twin_hop = hop(leaves(probes_hbm, twin_base, half), into_d(mine, 0, half), 3, me, twin)
+    ring_hop = hop(leaves(probes_hbm, half, REACH), into_d(mine, half, REACH), 4, me, twin)
     twin_hop.start()
 
     @pl.when(mine == 1)
@@ -184,6 +192,12 @@
 
     def both(field, k):
         return jnp.concatenate([field[0, k], field[1, k]], axis=0)
+
+    def probe_rows(r, k):
+        return d[r, :, pl.ds(pl.multiple_of(k * width, width), width)]
+
+    def both_probes(k):
+        return jnp.concatenate([probe_rows(0, k), probe_rows(1, k)], axis=0)
 
     def stack(k, x):
         hi = x.astype(BF16)
@@ -259,7 +273,7 @@
                 for c in range(3)
             ]
             top = jnp.broadcast_to(listed, (ROWS, 128))
-            for a in range(0, width, ROWS):
+            for a in range(0, width if o > 0 else at.stop, ROWS):
                 dx = pcb[0, a : a + ROWS, :] - right[0]
                 dy = pcb[1, a : a + ROWS, :] - right[1]
                 dz = pcb[2, a : a + ROWS, :] - right[2]
@@ -270,34 +284,51 @@
                 hi = t.astype(BF16)
                 tiles[s, 0, h, a : a + ROWS, :] = hi
                 tiles[s, 1, h, a : a + ROWS, :] = (t - hi.astype(F32)).astype(BF16)
-
-    for k in range(half):
-        d[mine, k] = own[base + k]
+            if o == 0:
+                for p in range(2):
+                    for g in range(h):
+                        block = tiles[s, p, h, g * 128 : g * 128 + 128, :]
+                        tiles[s, p, g, h * 128 : h * 128 + 128, :] = block.T
+
+    for copy in loads[3:]:
+        copy.wait()
 
     @pl.when(mine == 0)
     def _():
-        for k in range(half, span):
-            d[0, k] = own[k]
+        ring_load.wait()
 
     @pl.when(jnp.logical_and(mine == 1, me == n - 1))
     def _():
-        d[:, pl.ds(half, REACH)] = jnp.zeros((2, REACH, cols, width), F32)
+        d[:, :, half * width :] = jnp.zeros((2, cols, REACH * width), F32)
         prow[pl.ds(half, REACH)] = jnp.zeros((REACH, 8, width), F32)
 
     twin_hop.wait_recv()
     for k in range(half):
-        stack(k, both(d, k))
-
-    edge_hop = hop(acc.at[:, pl.ds(edge, REACH)], in_edge, 5, edge_leaf, twin)
+        stack(k, both_probes(k))
+
+    edge_hops = []
+    for j in range(REACH):
+        seat = jnp.where(mine == 0, j, REACH - 1 - j)
+        edge_hops.append(
+            pltpu.make_async_remote_copy(
+                src_ref=acc.at[:, edge + seat], dst_ref=in_edge.at[:, seat],
+                send_sem=esend.at[seat], recv_sem=erecv.at[seat],
+                device_id={"leaf": edge_leaf, "probe": twin}, device_id_type=MESH,
+            )
+        )
     inner_hop = hop(acc.at[:, pl.ds(inner, REACH)], in_twin, 6, me, twin)
     lag = half - REACH
 
+    def leaf_at(t):
+        late = jnp.where(t < AHEAD + REACH, half - 1 + AHEAD - t, t - REACH)
+        return jnp.where(mine == 0, t, jnp.where(t < AHEAD, t, late))
+
+    turn(0)
+
     def first_pass(t, carry):
-        i = jnp.where(
-            mine == 0, t, jnp.where(t < AHEAD, t, jnp.where(t < AHEAD + REACH, t + lag - AHEAD, t - REACH))
-        )
-
-        @pl.when(i == lag)
+        i = leaf_at(t)
+
+        @pl.when(t == jnp.where(mine == 0, lag, AHEAD))
         def _():
             @pl.when(mine == 0)
             def _():
@@ -310,26 +341,28 @@
                     rim_in[k].wait_recv()
 
             for k in range(half, span):
-                stack(k, both(d, k))
+                stack(k, both_probes(k))
 
         for j in range(len(steps) - 1):
-            @pl.when(t == 2 * j + 1)
+            @pl.when(t == j + 2)
             def _(j=j):
                 hear(j)
                 tell(j + 1)
 
-        turn(i)
         products(i, acc, build)
-
-        @pl.when(jnp.logical_and(t == REACH - 1 + AHEAD * mine, has_edge))
-        def _():
-            edge_hop.start()
+        turn(leaf_at(jnp.minimum(t + 1, half - 1)))
+
+        for j in range(REACH):
+
+            @pl.when(jnp.logical_and(t == j + AHEAD * mine, has_edge))
+            def _(j=j):
+                edge_hops[j].start()
 
         return carry
 
     lax.fori_loop(0, half, first_pass, 0)
     inner_hop.start()
-    for j in range(half // 2, len(steps) - 1):
+    for j in range(half - 2, len(steps) - 1):
         hear(j)
         tell(j + 1)
 
@@ -343,7 +376,7 @@
             x = acc[r, k]
             if more is not None:
                 x = x + more[r]
-            x = NORM * x - d[r, k]
+            x = NORM * x - probe_rows(r, k)
             w[r, k] = x
             xs.append(x)
         stack(k, jnp.concatenate(xs, axis=0))
@@ -353,7 +386,8 @@
 
     @pl.when(has_edge)
     def _():
-        edge_hop.wait_recv()
+        for copy in edge_hops:
+            copy.wait_recv()
 
     for k in range(REACH):
         make_w(edge + k, [in_edge[r, k] for r in range(2)])
@@ -391,6 +425,8 @@
 
         return carry
 
+    hear(len(steps) - 1)
+    greet(line_done, me, twin)
     lax.fori_loop(0, REACH, first_half, 0)
 
     def lanes(x):
@@ -404,7 +440,7 @@
         if k < half:
             own_part = own_part + wk * diag[k]
         if k < half:
-            dk = both(d, k)
+            dk = both_probes(k)
             sums[0] = sums[0] + dk * dk
             sums[1] = sums[1] + dk * wk
             sums[2] = sums[2] + wk * wk
@@ -413,8 +449,6 @@
     parts = three(stacked, 1)
     total = dot(jnp.full((8, parts.shape[1]), 1.0, BF16), parts, 1, 1)
     sum_out[...] = total[0:1]
-    hear(len(steps) - 1)
-    greet(line_done, me, twin)
     pl.semaphore_wait(line_done, 1)
     copies = []
     for slot, leaf, row in peers:
@@ -449,10 +483,10 @@
     for slot, copy in enumerate(copies):
         copy.wait_recv()
         total = total + sum_in[slot]
-    seat = lax.broadcasted_iota(jnp.int32, (cols, 128), 1)
+    column = lax.broadcasted_iota(jnp.int32, (cols, 128), 1)
     line = lax.broadcasted_iota(jnp.int32, (cols, 128), 0) + mine * cols
     rr, dw, ww, wk = [
-        jnp.sum(jnp.where(seat == line + q * rows, total, 0.0), axis=1, keepdims=True)
+        jnp.sum(jnp.where(column == line + q * rows, total, 0.0), axis=1, keepdims=True)
         for q in range(4)
     ]
     wz = NORM * wk - ww
@@ -485,8 +519,10 @@
 
     def finish(l, dl, wl, zl):
         at = pl.ds(pl.multiple_of(l * width, width), width)
-        sol_ref[:, at] = sol_d * dl - both_alpha * wl
-        res_ref[:, at] = res_d * dl + res_w * wl + res_z * zl
+        out_ref[0, :, at] = sol_d * dl
+        out_ref[1, :, at] = both_alpha * wl
+        out_ref[2, :, at] = res_d * dl + res_w * wl
+        out_ref[3, :, at] = res_z * zl
 
     for k in range(half):
         near = acc2[mine, k]
@@ -494,8 +530,8 @@
         if k < REACH:
             near = near + part[half + k]
             far = far + back[k]
-        finish(base + k, d[mine, k], w[mine, k], near)
-        finish(twin_base + k, own[twin_base + k], wfar[k], far)
+        finish(base + k, probe_rows(mine, k), w[mine, k], near)
+        finish(twin_base + k, own[:, k * width : (k + 1) * width], wfar[k], far)
 
     for copy in copies:
         copy.wait_send()
@@ -520,7 +556,8 @@
 
     @pl.when(has_edge)
     def _():
-        edge_hop.wait_send()
+        for copy in edge_hops:
+            copy.wait_send()
 
     @pl.when(jnp.logical_and(mine == 1, me < n - 1))
     def _():
@@ -539,22 +576,22 @@
     hbm = pl.BlockSpec(memory_space=pltpu.HBM)
     vmem = pl.BlockSpec(memory_space=pltpu.VMEM)
     field = functools.partial(pltpu.VMEM, dtype=F32)
-    return pl.pallas_call(
+    terms = pl.pallas_call(
         functools.partial(kernel, n),
-        out_shape=(jax.ShapeDtypeStruct(probes.shape, F32),) * 2,
+        out_shape=jax.ShapeDtypeStruct((4, *probes.shape), F32),
         in_specs=[hbm] * 4,
-        out_specs=(vmem, vmem),
+        out_specs=vmem,
         scratch_shapes=[
             field(coords.shape),
             pltpu.VMEM(site_order.shape, jnp.int32),
             pltpu.VMEM(leaf_pairs.shape, jnp.int32),
-            field((leaf_dev, cols, width)),
+            field((cols, half * width)),
             field((8, leaf_dev * width)),
             field((span, 8, width)),
             field((3, width, 128)),
             field((half * OFFS, 128)),
             pltpu.VMEM((half * OFFS, 2, width // 128, width, 128), BF16),
-            field((2, span, cols, width)),
+            field((2, cols, span * width)),
             field((2, span, cols, width)),
             field((half, cols, width)),
             pltpu.VMEM((span, 4 * cols, width), BF16),
@@ -567,19 +604,23 @@
             field((half, 2 * cols, width)),
             field((1, 128)),
             field((slots_in, 1, 128)),
-            pltpu.SemaphoreType.REGULAR((2 * n.bit_length(),)),
+            pltpu.SemaphoreType.REGULAR((2 * n.bit_length() + 2,)),
             pltpu.SemaphoreType.REGULAR,
-            pltpu.SemaphoreType.DMA((3 + leaf_dev,)),
+            pltpu.SemaphoreType.DMA((6,)),
             pltpu.SemaphoreType.DMA((slots_in,)),
             pltpu.SemaphoreType.DMA((slots_in,)),
             pltpu.SemaphoreType.DMA((11,)),
             pltpu.SemaphoreType.DMA((11,)),
+            pltpu.SemaphoreType.DMA((REACH,)),
+            pltpu.SemaphoreType.DMA((REACH,)),
         ],
         compiler_params=pltpu.CompilerParams(
             collective_id=0, has_side_effects=True, vmem_limit_bytes=48 * 2**20
         ),
     )(*[pltpu.with_memory_space_constraint(x, pltpu.HBM) for x in arrays])
 
+    return terms[0] - terms[1], terms[2] + terms[3]
+
 
 def solution(mesh):
     in_specs = (P(None, "leaf"), P("leaf", None), P(None, "leaf"), P("leaf"), P("probe", "leaf"))

time: 32.2 us -> 30.8 us (0.957)
  local copies, waits for them, and re-layouts: 1.41 us -> 0 us
  other arithmetic: 0 us -> 0.84 us
  Pallas kernels: 30 us -> 29.2 us
    unnamed x2 -> x0, local copies, waits for them, and re-layouts: 1.41 us -> none
    add x0 -> x1, other arithmetic: none -> 0.84 us  [body(): return (terms[0] - terms[1], terms[2] + terms[3])]
    pallas_call x1, Pallas kernels: 30 us -> 29.2 us  [body(): pl.pallas_call(functools.partial(kernel, n), out_shape=jax.ShapeDtypeStru...]
where the time goes in v4:
time: 30.8 us; the launch traced here: 30.7 us
  Pallas kernels  29.2 us (95%)
  other arithmetic  0.84 us (3%)
  between operations  0.64 us (2%)
    pallas_call x1, Pallas kernels, body(): pl.pallas_call(functools.partial(kernel, n), out_shape=jax.ShapeDtypeStru...  29.2 us
    add x1, other arithmetic, body(): return (terms[0] - terms[1], terms[2] + terms[3])  0.84 us

profile of v4, /device:TPU:0, one launch (start us, length us, event | category | flops | bytes accessed | tf_op | source)
XLA Modules:
  0.0 30.7 jit_solution(4335519043832909229)
XLA Ops:
  0.6 29.2 %shard_map.59 = f32[4,16,4096]{2,1,0:T(8,128)S(1)} custom-call(f32[3,4096]{1,0:T(4,128)} %coords_hbm.1, s32[16,256]{1,0:T(8,128)} %order_hbm.1, s32[2,96]{1,0:T(2,128)} %pairs_hbm.1, f32[16,4096]{1,0:T(8,128)} %probes_hbm.1), custom_call_target="tpu_custom_call" | custom-call | tf_op jit(solution)/shard_map/pallas_call | solution.py:579
  29.8 0.8 %add_bitcast_fusion = (f32[16,4096]{1,0:T(8,128)}, f32[16,4096]{1,0:T(8,128)}) fusion(f32[4,16,4096]{2,1,0:T(8,128)S(1)} %shard_map.59), kind=kLoop, calls=%fused_computation | loop fusion | flops 131072 | bytes 1572864 | tf_op jit(solution)/shard_map/add | solution.py:622

commit v5 on v4

--- a/solution.py
+++ b/solution.py
@@ -221,19 +221,20 @@
 
     def products(i, into, make):
         vi = v2[i]
-        cut = width // 2
-        row = [jnp.zeros((cut, 2 * rows), F32) for _ in range(2)]
-        for o in range(OFFS):
+        row = jnp.zeros((2 * rows, width), F32)
+        low = jnp.zeros((rows, width), F32)
+        for o in [*range(1, OFFS), 0]:
             make(i, o)
             hi, lo = tile(i * OFFS + o)
             vj = v2[i + o]
-            for q in range(2):
-                at = slice(q * cut, q * cut + cut)
-                row[q] = row[q] + dot(hi[at], vj, 1, 1) + dot(lo[at], vj, 1, 1)
             if o > 0:
                 add(into, i + o, columns(vi, hi, lo))
-        row = jnp.concatenate([x.T for x in row], axis=1)
-        add(into, i, row[:rows] + row[rows:])
+                row = row + dot(vj, hi, 1, 1)
+                low = low + dot(vj[:rows], lo, 1, 1)
+            else:
+                row = row + dot(vj, hi, 1, 0)
+                low = low + dot(vj[:rows], lo, 1, 0)
+        add(into, i, row[:rows] + row[rows:] + low)
 
     def first_products(i):
         vi = v2[i]

time: 30.8 us -> 30.3 us (0.984)
  Pallas kernels: 29.2 us -> 28.7 us
    pallas_call x1, Pallas kernels: 29.2 us -> 28.7 us  [body(): pl.pallas_call(functools.partial(kernel, n), out_shape=jax.ShapeDtypeStru...]
where the time goes in v5:
time: 30.3 us; the launch traced here: 30.2 us
  Pallas kernels  28.7 us (95%)
  other arithmetic  0.84 us (3%)
  between operations  0.64 us (2%)
    pallas_call x1, Pallas kernels, body(): pl.pallas_call(functools.partial(kernel, n), out_shape=jax.ShapeDtypeStru...  28.7 us
    add x1, other arithmetic, body(): return (terms[0] - terms[1], terms[2] + terms[3])  0.84 us

profile of v5, /device:TPU:0, one launch (start us, length us, event | category | flops | bytes accessed | tf_op | source)
XLA Modules:
  0.0 30.2 jit_solution(3223124675347544702)
XLA Ops:
  0.6 28.7 %shard_map.59 = f32[4,16,4096]{2,1,0:T(8,128)S(1)} custom-call(f32[3,4096]{1,0:T(4,128)} %coords_hbm.1, s32[16,256]{1,0:T(8,128)} %order_hbm.1, s32[2,96]{1,0:T(2,128)} %pairs_hbm.1, f32[16,4096]{1,0:T(8,128)} %probes_hbm.1), custom_call_target="tpu_custom_call" | custom-call | tf_op jit(solution)/shard_map/pallas_call | solution.py:580
  29.3 0.8 %add_bitcast_fusion = (f32[16,4096]{1,0:T(8,128)}, f32[16,4096]{1,0:T(8,128)}) fusion(f32[4,16,4096]{2,1,0:T(8,128)S(1)} %shard_map.59), kind=kLoop, calls=%fused_computation | loop fusion | flops 131072 | bytes 1572864 | tf_op jit(solution)/shard_map/add | solution.py:623

commit v6 on v5

--- a/solution.py
+++ b/solution.py
@@ -397,7 +397,7 @@
         first_products(t + REACH * mine)
         return carry
 
-    lax.fori_loop(0, lag, outer_columns, 0)
+    lax.fori_loop(0, lag, outer_columns, 0, unroll=True)
     inner_hop.wait_recv()
     for k in range(REACH):
         make_w(inner + k, [in_twin[r, k] for r in range(2)])
@@ -411,24 +411,21 @@
 
     left = lag * other
 
-    def first_half(t, carry):
-        i = left + REACH - 1 - t
-        first_products(i)
-
-        @pl.when(jnp.logical_and(i == lag, mine == 0))
-        def _():
-            give_rim.start()
-
-        @pl.when(jnp.logical_and(i == lag, jnp.logical_and(mine == 1, me < n - 1)))
-        def _():
-            next_even.start()
-            next_odd.start()
-
-        return carry
-
     hear(len(steps) - 1)
     greet(line_done, me, twin)
-    lax.fori_loop(0, REACH, first_half, 0)
+    for t in range(REACH):
+        first_products(left + REACH - 1 - t)
+        if t == 2 * REACH - half - 1:
+
+            @pl.when(jnp.logical_and(mine == 1, me < n - 1))
+            def _():
+                next_even.start()
+                next_odd.start()
+
+    @pl.when(mine == 0)
+    def _():
+        give_rim.start()
+
 
     def lanes(x):
         return x[:, :128] + x[:, 128:] if width == 256 else x
@@ -465,7 +462,7 @@
         last_products(i)
         return carry
 
-    lax.fori_loop(0, half, last_half, 0)
+    lax.fori_loop(0, half, last_half, 0, unroll=2)
     give_hop.start()
 
     @pl.when(jnp.logical_and(mine == 0, me == 0))

time: 30.3 us -> 30.1 us (level)
  no operation moved by 1% of the time
where the time goes in v6:
time: 30.1 us; the launch traced here: 29.9 us
  Pallas kernels  28.4 us (94%)
  other arithmetic  0.84 us (3%)
  between operations  0.64 us (2%)
    pallas_call x1, Pallas kernels, body(): pl.pallas_call(functools.partial(kernel, n), out_shape=jax.ShapeDtypeStru...  28.4 us
    add x1, other arithmetic, body(): return (terms[0] - terms[1], terms[2] + terms[3])  0.84 us

profile of v6, /device:TPU:0, one launch (start us, length us, event | category | flops | bytes accessed | tf_op | source)
XLA Modules:
  0.0 29.9 jit_solution(10483547386814152264)
XLA Ops:
  0.6 28.4 %shard_map.59 = f32[4,16,4096]{2,1,0:T(8,128)S(1)} custom-call(f32[3,4096]{1,0:T(4,128)} %coords_hbm.1, s32[16,256]{1,0:T(8,128)} %order_hbm.1, s32[2,96]{1,0:T(2,128)} %pairs_hbm.1, f32[16,4096]{1,0:T(8,128)} %probes_hbm.1), custom_call_target="tpu_custom_call" | custom-call | tf_op jit(solution)/shard_map/pallas_call | solution.py:577
  29.1 0.8 %add_bitcast_fusion = (f32[16,4096]{1,0:T(8,128)}, f32[16,4096]{1,0:T(8,128)}) fusion(f32[4,16,4096]{2,1,0:T(8,128)S(1)} %shard_map.59), kind=kLoop, calls=%fused_computation | loop fusion | flops 131072 | bytes 1572864 | tf_op jit(solution)/shard_map/add | solution.py:620
